TPU v7x, 16 devices: a 4x2x1 block of a 4x4x8 slice. The times are simulated.
16 devices in a mesh: dp: 2 (over y, z), sp: 8 (over x, core).
Axes of the slice: x: 4, y: 2, z: 1, core: 2. Of those that a mesh axis runs over, the one named last changes fastest.
The devices are a block of a 4x4x8 slice.
Arguments:
- patches: bfloat16 [16384, 1280], P(('dp', 'sp')), parts along dimension 0
- embeds: bfloat16 [8192, 2560], P(('dp', 'sp')), parts along dimension 0
- dest_slot: int32 [4096], P(('dp', 'sp')), parts along dimension 0
- rope_pos: int32 [3, 8192], P(None, ('dp', 'sp')), parts along dimension 1
- cu_doc: int32 [6], P('dp'), parts along dimension 0
- ln_w: bfloat16 [1280], replicated
- ln_b: bfloat16 [1280], replicated
- w_one: bfloat16 [5120, 5120], replicated
- b_one: bfloat16 [5120], replicated
- w_two: bfloat16 [5120, 2560], replicated
- b_two: bfloat16 [2560], replicated
- norm_attn: bfloat16 [2560], replicated
- w_q: bfloat16 [2560, 2560], replicated
- b_q: bfloat16 [2560], replicated
- w_k: bfloat16 [2560, 2560], replicated
- b_k: bfloat16 [2560], replicated
- w_v: bfloat16 [2560, 2560], replicated
- b_v: bfloat16 [2560], replicated
- w_o: bfloat16 [2560, 2560], replicated
- norm_mlp: bfloat16 [2560], replicated
- w_gate: bfloat16 [2560, 6912], replicated
- w_up: bfloat16 [2560, 6912], replicated
- w_down: bfloat16 [6912, 2560], replicated
Outputs:
- output: bfloat16 [8192, 2560], P(('dp', 'sp')), parts along dimension 0
There are 2 independent parts. A program takes and returns all parts, laid end to end along the dimension named above; an argument that names none is the same for every part.
All inputs are finite; a program needn't handle non-finite values.
Results may differ from a plain program's by a relative error of at most 0.0106714.
Values are sent between devices in bfloat16 or wider.
A program may use at most 768 MiB of HBM per device.

v0:
```python
import jax
import jax.numpy as jnp
from jax import lax
from jax.sharding import PartitionSpec as P

HEAD_DIM = 128
NORM_EPS = 1e-6
ROPE_THETA = 1000000.0
MROPE_SPLIT = (16, 40)


def layer_norm(values_in, gain_vec, shift_vec):
    widened = values_in.astype(jnp.float32)
    centered = widened - jnp.mean(widened, axis=-1, keepdims=True)
    spread = jnp.mean(centered * centered, axis=-1, keepdims=True)
    return (centered * lax.rsqrt(spread + NORM_EPS) * gain_vec.astype(jnp.float32) + shift_vec.astype(jnp.float32)).astype(jnp.bfloat16)


def rms_norm(values_in, gain_vec):
    widened = values_in.astype(jnp.float32)
    return (widened * lax.rsqrt(jnp.mean(widened * widened, axis=-1, keepdims=True) + NORM_EPS) * gain_vec.astype(jnp.float32)).astype(jnp.bfloat16)


def merger_mlp(grouped, w_one, b_one, w_two, b_two):
    inner = jax.nn.gelu(jnp.dot(grouped, w_one, preferred_element_type=jnp.float32) + b_one.astype(jnp.float32), approximate=False).astype(jnp.bfloat16)
    return (jnp.dot(inner, w_two, preferred_element_type=jnp.float32) + b_two.astype(jnp.float32)).astype(jnp.bfloat16)


def rope_tables(rope_pos):
    inv_freq = ROPE_THETA ** (-jnp.arange(0, HEAD_DIM, 2, dtype=jnp.float32) / HEAD_DIM)
    freq_idx = jnp.arange(HEAD_DIM // 2)[None, :]
    chosen = jnp.where(freq_idx < MROPE_SPLIT[0], rope_pos[0][:, None], jnp.where(freq_idx < MROPE_SPLIT[1], rope_pos[1][:, None], rope_pos[2][:, None]))
    angles = chosen.astype(jnp.float32) * inv_freq[None, :]
    angles = jnp.concatenate([angles, angles], axis=-1)
    return jnp.cos(angles), jnp.sin(angles)


def apply_rope(heads_in, cos_t, sin_t):
    half_dim = HEAD_DIM // 2
    rotated = jnp.concatenate([-heads_in[..., half_dim:], heads_in[..., :half_dim]], axis=-1)
    return heads_in * cos_t[:, None, :] + rotated * sin_t[:, None, :]


def qkv_project(normed_a, rope_pos, w_q, b_q, w_k, b_k, w_v, b_v):
    tokens = normed_a.shape[0]
    cos_t, sin_t = rope_tables(rope_pos)
    q_lin = jnp.dot(normed_a, w_q, preferred_element_type=jnp.float32) + b_q.astype(jnp.float32)
    k_lin = jnp.dot(normed_a, w_k, preferred_element_type=jnp.float32) + b_k.astype(jnp.float32)
    queries = apply_rope(q_lin.reshape(tokens, -1, HEAD_DIM), cos_t, sin_t).astype(jnp.bfloat16)
    keys_rot = apply_rope(k_lin.reshape(tokens, -1, HEAD_DIM), cos_t, sin_t).astype(jnp.bfloat16)
    values_bf = (jnp.dot(normed_a, w_v, preferred_element_type=jnp.float32) + b_v.astype(jnp.float32)).astype(jnp.bfloat16).reshape(tokens, -1, HEAD_DIM)
    return queries, keys_rot, values_bf


def mlp_residual(h_one, norm_mlp, w_gate, w_up, w_down):
    normed_m = rms_norm(h_one, norm_mlp)
    gate_pre = jnp.dot(normed_m, w_gate, preferred_element_type=jnp.float32)
    up_pre = jnp.dot(normed_m, w_up, preferred_element_type=jnp.float32)
    activated = (jax.nn.silu(gate_pre) * up_pre).astype(jnp.bfloat16)
    return (h_one.astype(jnp.float32) + jnp.dot(activated, w_down, preferred_element_type=jnp.float32)).astype(jnp.bfloat16)


def solution(mesh):
    group_size = mesh.shape['sp']
    row_spec = P(('dp', 'sp'), None)

    def local_step(patches, embeds, dest_slot, rope_pos, cu_doc, ln_w, ln_b, w_one, b_one, w_two, b_two, norm_attn, w_q, b_q, w_k, b_k, w_v, b_v, w_o, norm_mlp, w_gate, w_up, w_down):
        tok_dev = embeds.shape[0]
        merged_dev = dest_slot.shape[0]
        my_shard = lax.axis_index('sp')
        normed = layer_norm(patches, ln_w, ln_b).reshape(merged_dev, -1)
        merged = merger_mlp(normed, w_one, b_one, w_two, b_two)
        to_shard = dest_slot // tok_dev
        send_mask = to_shard[None, :] == jnp.arange(group_size)[:, None]
        send_buf = jnp.where(send_mask[:, :, None], merged[None, :, :], 0)
        received = lax.all_to_all(send_buf, 'sp', 0, 0, tiled=True).reshape(group_size * merged_dev, -1)
        all_slots = lax.all_gather(dest_slot, 'sp', tiled=True)
        pick_mask = all_slots[None, :] == (my_shard * tok_dev + jnp.arange(tok_dev))[:, None]
        placed = jnp.dot(pick_mask.astype(jnp.bfloat16), received, preferred_element_type=jnp.float32).astype(jnp.bfloat16)
        h_zero = jnp.where(jnp.any(pick_mask, axis=1)[:, None], placed, embeds)
        queries, keys_loc, values_loc = qkv_project(rms_norm(h_zero, norm_attn), rope_pos, w_q, b_q, w_k, b_k, w_v, b_v)
        keys_all = lax.all_gather(keys_loc, 'sp', tiled=True)
        values_all = lax.all_gather(values_loc, 'sp', tiled=True)
        seq_len = group_size * tok_dev
        doc_cuts = cu_doc[1:-1]
        key_pos = jnp.arange(seq_len)
        query_pos = my_shard * tok_dev + jnp.arange(tok_dev)
        key_doc = jnp.sum(key_pos[:, None] >= doc_cuts[None, :], axis=1)
        query_doc = jnp.sum(query_pos[:, None] >= doc_cuts[None, :], axis=1)
        allowed = (key_pos[None, :] <= query_pos[:, None]) & (query_doc[:, None] == key_doc[None, :])
        grouped_q = queries.reshape(tok_dev, keys_loc.shape[1], -1, HEAD_DIM)
        scores = jnp.einsum('qkgd,tkd->kgqt', grouped_q, keys_all, preferred_element_type=jnp.float32) * HEAD_DIM ** -0.5
        probs_bf = jax.nn.softmax(jnp.where(allowed, scores, -1e30), axis=-1).astype(jnp.bfloat16)
        attn_out = jnp.einsum('kgqt,tkd->qkgd', probs_bf, values_all, preferred_element_type=jnp.float32).astype(jnp.bfloat16).reshape(tok_dev, -1)
        h_one = (h_zero.astype(jnp.float32) + jnp.dot(attn_out, w_o, preferred_element_type=jnp.float32)).astype(jnp.bfloat16)
        return mlp_residual(h_one, norm_mlp, w_gate, w_up, w_down)

    in_specs = (row_spec, row_spec, P(('dp', 'sp')), P(None, ('dp', 'sp')), P('dp')) + (P(),) * 18
    return jax.shard_map(local_step, mesh=mesh, in_specs=in_specs, out_specs=row_spec, check_vma=False)
```

profile of v0, /device:TPU:113, one launch (start us, length us, event | category | flops | bytes accessed | tf_op | source)
XLA Modules:
  0.0 633.8 jit_solution(3629178415986075418)
XLA Ops:
  6.6 2.3 convert_reduce_fusion
  8.9 2.6 fusion.9
  11.5 1.0 fusion.12
  12.6 2.9 reshape.260
  15.5 43.9 %fusion.38 = bf16[256,2560]{1,0:T(8,128)(2,1)S(1)} fusion(bf16[5120,2560]{1,0:T(8,128)(2,1)} %param.32, bf16[256,5120]{1,0:T(8,128)(2,1)} %reshape.260, bf16[5120,5120]{1,0:T(8,128)(2,1)} %param.30, f32[5120]{0:T(1024)S(1)} %convert_element_type.121, f32[2560]{0:T(1024)S(1)} %convert_element_type.123), kind=kOutput, calls=%fused_computation.69 | convolution fusion | flops 20220477440 | bytes 82606080 | tf_op jit(solution)/shard_map/dot_general | solution.py:26
  59.4 4.6 broadcast_select_fusion
  64.1 6.1 all-to-all-start
  70.3 126.2 %all-gather = s32[8,1,256]{2,1,0:T(1,128)S(1)} all-gather(s32[1,1,256]{2,1,0:T(1,128)S(1)} %bitcast.73), channel_id=1, replica_groups=mesh['dp'=2,'sp'=8] {'sp'}, dimensions={0}, use_global_device_ids=true | all-gather | bytes 9216 | tf_op jit(solution)/shard_map/all_gather | solution.py:77
  196.8 1.1 fusion.87
  198.6 10.7 %fusion.16 = (f32[512]{0:T(512)S(1)}, bf16[512,2560]{1,0:T(8,128)(2,1)S(1)}) fusion(bf16[512,2560]{1,0:T(8,128)(2,1)} %param.24, bf16[2048,2560]{1,0:T(8,128)(2,1)} %bitcast.2, s32[2048]{0:T(1024)S(1)} %bitcast.69, s32[512]{0:T(512)S(1)} %iota_add_fusion, pred[512]{0:T(512)(128)(4,1)S(1)} %compare_reduce_fusion), kind=kOutput, calls=%fused_computation.33 | convolution fusion | flops 5376310784 | bytes 15741440 | tf_op jit(solution)/shard_map/dot_general | solution.py:79
  209.4 1.5 copy-done.17
  210.9 11.7 %convolution_add_fusion.2 = f32[512,2560]{1,0:T(8,128)} fusion(bf16[2560,2560]{1,0:T(8,128)(2,1)} %param.37, f32[2560]{0:T(1024)S(1)} %convert_element_type.133, bf16[512,2560]{1,0:T(8,128)(2,1)S(1)} %get-tuple-element.15, f32[2560]{0:T(1024)S(1)} %convert_element_type.127, f32[512]{0:T(512)S(1)} %add_rsqrt_fusion.2), kind=kOutput, calls=%fused_computation.66 | convolution fusion | flops 6717440000 | bytes 20994048 | tf_op jit(solution)/shard_map/dot_general | solution.py:48
  222.5 5.9 copy.53
  228.4 5.9 copy.54
  234.4 8.4 %slice_negate_fusion.1 = (f32[512,20,64]{2,0,1:T(8,128)S(1)}, f32[512,20,64]{2,0,1:T(8,128)}) fusion(f32[512,20,128]{2,0,1:T(8,128)} %copy.54), kind=kLoop, calls=%fused_computation.42 | loop fusion | flops 655360 | bytes 10485760 | tf_op jit(solution)/shard_map/neg | solution.py:40
  242.8 5.5 fusion.25
  248.8 10.9 %add_convert_fusion = bf16[512,2560]{1,0:T(8,128)(2,1)S(1)} fusion(bf16[2560,2560]{1,0:T(8,128)(2,1)} %param.39, f32[2560]{0:T(1024)S(1)} %convert_element_type.129, bf16[512,2560]{1,0:T(8,128)(2,1)} %copy-done.17, f32[2560]{0:T(1024)S(1)} %convert_element_type.127, f32[512]{0:T(512)S(1)} %add_rsqrt_fusion.2), kind=kOutput, calls=%fused_computation.49 | convolution fusion | flops 6718750720 | bytes 18372608 | tf_op jit(solution)/shard_map/dot_general | solution.py:51
  259.8 2.7 copy.52
  265.2 2.2 fusion.4
  267.4 12.4 %convolution_add_fusion.1 = f32[512,2560]{1,0:T(8,128)} fusion(bf16[2560,2560]{1,0:T(8,128)(2,1)} %param.35, f32[2560]{0:T(1024)S(1)} %convert_element_type.136, bf16[512,2560]{1,0:T(8,128)(2,1)} %copy-done.17, f32[2560]{0:T(1024)S(1)} %convert_element_type.127, f32[512]{0:T(512)S(1)} %add_rsqrt_fusion.2), kind=kOutput, calls=%fused_computation.65 | convolution fusion | flops 6717440000 | bytes 20994048 | tf_op jit(solution)/shard_map/dot_general | solution.py:47
  279.8 5.9 copy.57
  285.7 5.9 copy.58
  291.7 8.4 %slice_negate_fusion = (f32[512,20,64]{2,0,1:T(8,128)S(1)}, f32[512,20,64]{2,0,1:T(8,128)}) fusion(f32[512,20,128]{2,0,1:T(8,128)} %copy.58), kind=kLoop, calls=%fused_computation.41 | loop fusion | flops 655360 | bytes 10485760 | tf_op jit(solution)/shard_map/neg | solution.py:40
  300.0 5.6 fusion.44.clone.4
  305.7 47.9 %all-gather.6.cloned.1.call-done = bf16[4096,20,128]{2,0,1:T(8,128)(2,1)} async-done(((bf16[512,20,128]{2,0,1:T(8,128)(2,1)}), bf16[4096,20,128]{2,0,1:T(8,128)(2,1)}) %all-gather.6.cloned.1.call-update) | async-done | bytes 20971536 | tf_op jit(solution)/shard_map/all_gather | solution.py:82
  353.6 64.7 %fusion.1 = (f32[20,512]{1,0:T(8,128)S(1)}, f32[20,4096,512]{2,1,0:T(8,128)}) fusion(pred[512,4096]{0,1:T(8,128)(4,1)S(1)} %fusion.4, bf16[4096,20,128]{2,0,1:T(8,128)(2,1)} %all-gather.6.cloned.1.call-done, bf16[512,20,128]{2,0,1:T(8,128)(2,1)} %fusion.44.clone.4), kind=kOutput, calls=%fused_computation.4 | convolution fusion | flops 10863237120 | bytes 193503232 | tf_op jit(solution)/shard_map/qkgd,tkd->kgqt/dot_general | solution.py:92
  418.3 51.0 %fusion = f32[20,512]{1,0:T(8,128)S(1)} fusion(f32[20,4096,512]{2,1,0:T(8,128)} %get-tuple-element.17, f32[20,512]{1,0:T(8,128)S(1)} %get-tuple-element.16, pred[512,4096]{0,1:T(8,128)(4,1)S(1)} %fusion.4), kind=kLoop, calls=%fused_computation.3 | loop fusion | flops 167761920 | bytes 169951232 | tf_op jit(solution)/shard_map/reduce_sum | solution.py:93
  469.4 65.2 %fusion.80 = bf16[20,128,512]{2,1,0:T(8,128)(2,1)} fusion(bf16[4096,20,128]{0,2,1:T(8,128)(2,1)} %all-gather.4.cloned.1.call-done, f32[20,512]{1,0:T(8,128)S(1)} %fusion, f32[20,512]{1,0:T(8,128)S(1)} %get-tuple-element.16, f32[20,4096,512]{2,1,0:T(8,128)} %get-tuple-element.17, pred[512,4096]{0,1:T(8,128)(4,1)S(1)} %fusion.4), kind=kOutput, calls=%fused_computation.107 | convolution fusion | flops 10948444160 | bytes 193544192 | tf_op jit(solution)/shard_map/kgqt,tkd->qkgd/dot_general | solution.py:94
  534.6 11.9 %fusion.20 = (f32[512]{0:T(512)S(1)}, bf16[512,2560]{1,0:T(8,128)(2,1)S(1)}) fusion(bf16[512,2560]{0,1:T(8,128)(2,1)} %bitcast.74, bf16[2560,2560]{1,0:T(8,128)(2,1)} %param.41, bf16[512,2560]{1,0:T(8,128)(2,1)} %copy-done.17), kind=kOutput, calls=%fused_computation.37 | convolution fusion | flops 6718750208 | bytes 20973568 | tf_op jit(solution)/shard_map/dot_general | solution.py:95
  546.5 25.4 %fusion.84 = f32[512,6912]{1,0:T(8,128)} fusion(bf16[2560,6912]{1,0:T(8,128)(2,1)} %param.43, bf16[512,2560]{1,0:T(8,128)(2,1)S(1)} %get-tuple-element.19, f32[2560]{0:T(1024)S(1)} %copy-done.4, f32[512]{0:T(512)S(1)} %add_rsqrt_fusion.1), kind=kOutput, calls=%fused_computation.108 | convolution fusion | flops 18124636160 | bytes 52178944 | tf_op jit(solution)/shard_map/dot_general | solution.py:57
  571.9 26.5 %fusion.160 = bf16[512,6912]{1,0:T(8,128)(2,1)} fusion(bf16[2560,6912]{1,0:T(8,128)(2,1)} %param.44, bf16[512,2560]{1,0:T(8,128)(2,1)S(1)} %get-tuple-element.19, f32[2560]{0:T(1024)S(1)} %copy-done.4, f32[512]{0:T(512)S(1)} %add_rsqrt_fusion.1, f32[512,6912]{1,0:T(8,128)} %fusion.84), kind=kOutput, calls=%bitcast_fusion.2.clone.1 | convolution fusion | flops 18145869824 | bytes 59256832 | tf_op jit(solution)/shard_map/dot_general | solution.py:58
  598.4 28.1 %fusion.23 = bf16[512,2560]{1,0:T(8,128)(2,1)} fusion(bf16[512,2560]{1,0:T(8,128)(2,1)S(1)} %get-tuple-element.19, bf16[6912,2560]{1,0:T(8,128)(2,1)} %param.45, bf16[512,6912]{1,0:T(8,128)(2,1)} %fusion.160), kind=kOutput, calls=%fused_computation.40 | convolution fusion | flops 18123325440 | bytes 47710208 | tf_op jit(solution)/shard_map/dot_general | solution.py:60
  (65 shorter events, 4.3 us)
Async XLA Ops:
  6.5 4.9 copy-start.2
  6.5 4.9 copy-start.13
  6.6 4.9 copy-start.14
  11.5 4.0 copy-start.5
  11.5 4.0 copy-start.6
  11.5 4.0 copy-start.15
  64.1 6.2 copy-start.7
  64.1 6.2 copy-start.8
  64.1 132.5 %copy-start.12 = (s32[3,512]{1,0:T(4,128)S(1)}, s32[3,512]{1,0:T(4,128)}, u32[]{:S(2)}) copy-start(s32[3,512]{1,0:T(4,128)} %param.26) | copy-start | bytes 18436
  64.1 134.5 %all-to-all-start = ((bf16[8,256,2560]{2,1,0:T(8,128)(2,1)}), bf16[8,256,2560]{2,1,0:T(8,128)(2,1)}, u32[]{:S(2)}, u32[]{:S(2)}) async-start(bf16[8,256,2560]{2,1,0:T(8,128)(2,1)} %broadcast_select_fusion), calls=%async_computation | async-start | bytes 20971520 | tf_op jit(solution)/shard_map/all_to_all | solution.py:76
  70.2 283.4 %all-gather.6.cloned.1.call-start = ((), (), s32[]{:S(2)}) async-start(), calls=%async_computation.2 | async-start | bytes 23592960 | tf_op jit(solution)/shard_map/all_gather | solution.py:82
  197.9 44.8 %copy-start.3 = (f32[512,128]{1,0:T(8,128)}, f32[512,128]{1,0:T(8,128)S(1)}, u32[]{:S(2)}) copy-start(f32[512,128]{1,0:T(8,128)S(1)} %get-tuple-element.10) | copy-start | bytes 786436
  209.4 1.5 copy-start.17
  234.4 8.4 %copy-start.1 = (f32[512,20,128]{2,0,1:T(8,128)S(1)}, f32[512,20,128]{2,0,1:T(8,128)}, u32[]{:S(2)}) copy-start(f32[512,20,128]{2,0,1:T(8,128)} %copy.54) | copy-start | bytes 15728644
  242.8 6.0 copy-start.9
  248.3 221.0 %all-gather.4.cloned.1.call-start = ((), (), s32[]{:S(2)}) async-start(), calls=%async_computation.1 | async-start | bytes 23592960 | tf_op jit(solution)/shard_map/all_gather | solution.py:83
  259.7 2.8 copy-start.10
  259.7 2.8 copy-start.16
  259.8 3.4 copy-start.11
  291.7 8.4 %copy-start = (f32[512,20,128]{2,0,1:T(8,128)S(1)}, f32[512,20,128]{2,0,1:T(8,128)}, u32[]{:S(2)}) copy-start(f32[512,20,128]{2,0,1:T(8,128)} %copy.58) | copy-start | bytes 15728644
  534.6 11.9 %copy-start.4 = (f32[2560]{0:T(1024)S(1)}, f32[2560]{0:T(1024)}, u32[]{:S(2)}) copy-start(f32[2560]{0:T(1024)} %convert_element_type.144) | copy-start | bytes 30724
Sparse Core Ops, SparseCore 0:
  248.4 105.1 all-gather.5
  355.2 99.5 all-gather.3
where the time goes:
time: 643 us; the launch traced here: 634 us
  matrix products  311 us (48%)
  blocking collectives  126 us (20%)
  other arithmetic  95.8 us (15%)
  waiting for transfers between devices  48 us (7%)
  local copies, waits for them, and re-layouts  31.5 us (5%)
  between operations  14.3 us (2%)
  starting transfers between devices  6.62 us (1%)
    all_gather x1, blocking collectives, local_step(): all_slots = lax.all_gather(dest_slot, 'sp', tiled=True)  126 us
    dot_general x1, matrix products, local_step(): jnp.einsum('kgqt,tkd->qkgd', probs_bf, values_all, preferred_element_type...  65.2 us
    dot_general x1, matrix products, local_step(): jnp.einsum('qkgd,tkd->kgqt', grouped_q, keys_all, preferred_element_type=...  64.7 us
    reduce_sum x1, other arithmetic, local_step(): jax.nn.softmax(jnp.where(allowed, scores, -1e+30), axis=-1)  51 us
    all_gather x1, waiting for transfers between devices, local_step(): keys_all = lax.all_gather(keys_loc, 'sp', tiled=True)  47.9 us
    dot_general x1, matrix products, merger_mlp(): jnp.dot(inner, w_two, preferred_element_type=jnp.float32)  43.9 us
    dot_general x1, matrix products, mlp_residual(): jnp.dot(activated, w_down, preferred_element_type=jnp.float32)  28.1 us
    dot_general x1, matrix products, mlp_residual(): up_pre = jnp.dot(normed_m, w_up, preferred_element_type=jnp.float32)  26.5 us
  transfers between devices with their start and end apart: 3, of which 1 were waited for; matrix products, arithmetic and copies ran while one was open for 28% of the time, Pallas kernels for 0%

commit v1 on v0

v1 whole, which is shorter than its diff:
```python
import functools

import jax
import jax.numpy as jnp
from jax import lax
from jax.experimental import pallas as pl
from jax.experimental.pallas import tpu as pltpu
from jax.sharding import PartitionSpec as P

HEAD_DIM = 128
NORM_EPS = 1e-6
ROPE_THETA = 1000000.0
MROPE_SPLIT = (16, 40)
CORES = 2
NEG_BIG = -1e30
LOG2_E = 1.4426950408889634
F32 = jnp.float32
BF16 = jnp.bfloat16
VMEM_LIMIT = 60 * 1024 * 1024


def cost(flops, nbytes, trans=0):
    return pl.CostEstimate(flops=int(flops), bytes_accessed=int(nbytes), transcendentals=int(trans))


def params(limit=VMEM_LIMIT):
    return pltpu.CompilerParams(vmem_limit_bytes=limit)


def dot32(lhs, rhs):
    return jnp.dot(lhs, rhs, preferred_element_type=F32)


def merger_kernel(x_ref, lnw_ref, lnb_ref, w1_ref, b1_ref, w2_ref, b2_ref, out_ref, wide_ref, z_ref, acc_ref):
    step = pl.program_id(0)
    rows, feat = out_ref.shape[0], x_ref.shape[1]

    @pl.when(step == 0)
    def _():
        x = x_ref[...].astype(F32)
        cent = x - jnp.mean(x, axis=-1, keepdims=True)
        var = jnp.mean(cent * cent, axis=-1, keepdims=True)
        normed = cent * lax.rsqrt(var + NORM_EPS) * lnw_ref[...].astype(F32) + lnb_ref[...].astype(F32)
        for j in range(feat // 128):
            wide_ref[j] = normed[:, j * 128:(j + 1) * 128]
        for i in range(4):
            for j in range(feat // 128):
                col = i * feat + j * 128
                z_ref[:, col:col + 128] = wide_ref[j, pl.ds(i, rows, stride=4), :].astype(BF16)
        acc_ref[...] = jnp.zeros_like(acc_ref)

    pre = dot32(z_ref[...], w1_ref[...]) + b1_ref[...].astype(F32)
    inner = (0.5 * pre * (1.0 + lax.erf(pre * 2.0 ** -0.5))).astype(BF16)
    acc_ref[...] += dot32(inner, w2_ref[...])

    @pl.when(step == pl.num_programs(0) - 1)
    def _():
        out_ref[...] = (acc_ref[...] + b2_ref[...].astype(F32)).astype(BF16)


def merger(patches, ln_w, ln_b, w_one, b_one, w_two, b_two):
    total, feat = patches.shape
    rows = total // 4
    depth, mid = w_one.shape
    hid = w_two.shape[1]
    tile = 512
    whole = lambda i: (0, 0)
    return pl.pallas_call(
        merger_kernel,
        grid=(mid // tile,),
        in_specs=[
            pl.BlockSpec((total, feat), whole),
            pl.BlockSpec((1, feat), whole),
            pl.BlockSpec((1, feat), whole),
            pl.BlockSpec((depth, tile), lambda i: (0, i)),
            pl.BlockSpec((1, tile), lambda i: (0, i)),
            pl.BlockSpec((tile, hid), lambda i: (i, 0)),
            pl.BlockSpec((1, hid), whole),
        ],
        out_specs=pl.BlockSpec((rows, hid), whole),
        out_shape=jax.ShapeDtypeStruct((rows, hid), BF16),
        scratch_shapes=[
            pltpu.VMEM((feat // 128, total, 128), F32),
            pltpu.VMEM((rows, depth), BF16),
            pltpu.VMEM((rows, hid), F32),
        ],
        compiler_params=params(),
        cost_estimate=cost(2 * rows * mid * (depth + hid), 2 * mid * (depth + hid)),
        name="merger",
    )(patches, ln_w[None], ln_b[None], w_one, b_one[None], w_two, b_two[None])


def place_kernel(info_ref, slots_ref, m_ref, placed_ref, mask_ref):
    step = pl.program_id(0)
    rows = placed_ref.shape[1]
    per_shard = info_ref[2] // rows
    base = info_ref[2] * (CORES * (step // per_shard) + info_ref[1]) + rows * (step % per_shard)
    pos = base + lax.broadcasted_iota(jnp.int32, (rows, slots_ref.shape[1]), 0)
    hit = (slots_ref[...] == pos).astype(F32)
    placed_ref[0] = dot32(hit.astype(BF16), m_ref[...]).astype(BF16)
    any_hit = jnp.max(hit, axis=1, keepdims=True)
    mask_ref[0] = jnp.broadcast_to(any_hit, mask_ref.shape[1:]).astype(BF16)


def place(info, slots, m_all, chips, tok):
    rows = 256
    hid = m_all.shape[1]
    per = tok // rows
    grid_spec = pltpu.PrefetchScalarGridSpec(
        num_scalar_prefetch=1,
        grid=(chips * per,),
        in_specs=[
            pl.BlockSpec((1, slots.shape[0]), lambda i, s: (0, 0)),
            pl.BlockSpec(m_all.shape, lambda i, s: (0, 0)),
        ],
        out_specs=[
            pl.BlockSpec((1, rows, hid), lambda i, s: (i // per, i % per, 0)),
            pl.BlockSpec((1, rows, 128), lambda i, s: (i // per, i % per, 0)),
        ],
    )
    return pl.pallas_call(
        place_kernel,
        grid_spec=grid_spec,
        out_shape=[jax.ShapeDtypeStruct((chips, tok, hid), BF16), jax.ShapeDtypeStruct((chips, tok, 128), BF16)],
        compiler_params=params(),
        cost_estimate=cost(2 * chips * tok * m_all.shape[0] * hid, 2 * m_all.size + 2 * chips * tok * hid),
        name="place",
    )(info, slots[None], m_all)


def qkv_kernel(info_ref, e_ref, p_ref, mask_ref, g_ref, cos_ref, sin_ref, bq_ref, bk_ref, bv_ref, wq_ref, wk_ref, wv_ref,
               q_ref, kv_ref, wq_buf, wk_buf, wv_buf, sems):
    width = wq_buf.shape[1]
    col = pl.multiple_of(info_ref[0] * width, width)
    first = pl.program_id(0) == 0
    pairs = ((wq_ref, wq_buf), (wk_ref, wk_buf), (wv_ref, wv_buf))

    def copy(i):
        src, dst = pairs[i]
        return pltpu.make_async_copy(src.at[:, pl.ds(col, width)], dst, sems.at[i])

    @pl.when(first)
    def _():
        for i in range(3):
            copy(i).start()

    chips, rows, hid = e_ref.shape
    flat = chips * rows
    hit = mask_ref[...].reshape(flat, 128)[:, :1].astype(F32) > 0.5
    h = jnp.where(hit, p_ref[...].reshape(flat, hid).astype(F32), e_ref[...].reshape(flat, hid).astype(F32))
    a = (h * lax.rsqrt(jnp.mean(h * h, axis=-1, keepdims=True) + NORM_EPS) * g_ref[...].astype(F32)).astype(BF16)
    cos_t = cos_ref[...].reshape(flat, HEAD_DIM)
    sin_t = sin_ref[...].reshape(flat, HEAD_DIM)

    def rope_to(lin, out_ref):
        for j in range(width // HEAD_DIM):
            cols = slice(j * HEAD_DIM, (j + 1) * HEAD_DIM)
            part = lin[:, cols]
            turned = part * cos_t + pltpu.roll(part, HEAD_DIM // 2, 1) * sin_t
            out_ref[:, :, cols] = turned.astype(BF16).reshape(chips, rows, HEAD_DIM)

    for i in range(3):
        @pl.when(first)
        def _():
            copy(i).wait()

        lin = dot32(a, pairs[i][1][...])
        if i == 0:
            rope_to(lin + bq_ref[...].astype(F32), q_ref)
        elif i == 1:
            rope_to(lin + bk_ref[...].astype(F32), kv_ref)
        else:
            v = (lin + bv_ref[...].astype(F32)).astype(BF16)
            kv_ref[:, :, width:] = v.reshape(chips, rows, width)


def qkv(info, e, placed, mask, cos_t, sin_t, norm, w_q, b_q, w_k, b_k, w_v, b_v, row0, width):
    chips, total, hid = e.shape
    rows = 128
    b0 = row0 // rows
    slab = lambda i, s: (0, i, 0)
    off = lambda i, s: (0, i + b0, 0)
    bias = pl.BlockSpec((1, width), lambda i, s: (0, s[0]))
    anyspec = pl.BlockSpec(memory_space=pl.ANY)
    grid_spec = pltpu.PrefetchScalarGridSpec(
        num_scalar_prefetch=1,
        grid=(total // rows,),
        in_specs=[
            pl.BlockSpec((chips, rows, hid), slab),
            pl.BlockSpec((chips, rows, hid), off),
            pl.BlockSpec((chips, rows, 128), off),
            pl.BlockSpec((1, hid), lambda i, s: (0, 0)),
            pl.BlockSpec((chips, rows, HEAD_DIM), off),
            pl.BlockSpec((chips, rows, HEAD_DIM), off),
            bias, bias, bias, anyspec, anyspec, anyspec,
        ],
        out_specs=[
            pl.BlockSpec((chips, rows, width), slab),
            pl.BlockSpec((chips, rows, 2 * width), slab),
        ],
        scratch_shapes=[pltpu.VMEM((hid, width), BF16)] * 3 + [pltpu.SemaphoreType.DMA((3,))],
    )
    return pl.pallas_call(
        qkv_kernel,
        grid_spec=grid_spec,
        out_shape=[jax.ShapeDtypeStruct((chips, total, width), BF16), jax.ShapeDtypeStruct((chips, total, 2 * width), BF16)],
        compiler_params=params(),
        cost_estimate=cost(2 * chips * total * hid * 3 * width, 2 * hid * 3 * width + 4 * chips * total * hid),
        name="qkv",
    )(info, e, placed, mask, norm[None], cos_t, sin_t, b_q[None], b_k[None], b_v[None], w_q, w_k, w_v)


def attn_kernel(num_docs, n_slab, *refs):
    info_ref = refs[0]
    q_refs = refs[1:1 + n_slab]
    groups = [refs[1 + n_slab * (1 + g):1 + n_slab * (2 + g)] for g in range(4)]
    k_own, v_own, k_sib, v_sib = groups
    o_ref, m_ref, l_ref, acc_ref = refs[1 + 5 * n_slab:]
    shard_chip, core = info_ref[0], info_ref[1]
    queries = o_ref.shape[0]
    q_base = queries * (CORES * shard_chip + core)
    q = jnp.concatenate([r[0] for r in q_refs], axis=0)
    q_pos = q_base + lax.broadcasted_iota(jnp.int32, (1, queries), 1)

    def doc_start(pos):
        start = jnp.zeros_like(pos)
        for d in range(1, num_docs):
            cut = info_ref[2 + d]
            start = jnp.where(pos >= cut, cut, start)
        return start

    starts = doc_start(q_pos)
    lo_start = doc_start(q_base)
    hi_start = doc_start(q_base + queries - 1)
    factor = HEAD_DIM ** -0.5 * LOG2_E
    halves = 2
    half = queries // halves

    def block(k_refs, v_refs, idx, k_base, masked, fresh):
        k = jnp.concatenate([r[idx] for r in k_refs], axis=0)
        v = jnp.concatenate([r[idx] for r in v_refs], axis=0)
        for i in range(halves):
            lanes = slice(i * half, (i + 1) * half)
            s = lax.dot_general(k, q[lanes], (((1,), (1,)), ((), ())), preferred_element_type=F32)
            if masked:
                k_pos = k_base + lax.broadcasted_iota(jnp.int32, s.shape, 0)
                s = jnp.where((k_pos <= q_pos[:, lanes]) & (k_pos >= starts[:, lanes]), s, NEG_BIG)
            top = jnp.max(s, axis=0, keepdims=True)
            if not fresh:
                old = m_ref[:, lanes]
                top = jnp.maximum(top, old)
            p = jnp.exp2((s - top) * factor)
            total = jnp.sum(p, axis=0, keepdims=True)
            out = lax.dot_general(v, p.astype(BF16), (((0,), (0,)), ((), ())), preferred_element_type=F32)
            if not fresh:
                alpha = jnp.exp2((old - top) * factor)
                total = total + l_ref[:, lanes] * alpha
                out = out + acc_ref[:, lanes] * alpha
            m_ref[:, lanes] = top
            l_ref[:, lanes] = total
            acc_ref[:, lanes] = out

    block(k_own, v_own, shard_chip, q_base, True, True)

    def sweep(k_refs, v_refs, parity, end):
        begin = (lo_start // queries - parity + 1) // CORES

        def body(j, carry):
            k_base = queries * (CORES * j + parity)

            @pl.when(k_base >= hi_start)
            def _():
                block(k_refs, v_refs, j, k_base, False, False)

            @pl.when(k_base < hi_start)
            def _():
                block(k_refs, v_refs, j, k_base, True, False)

            return carry

        lax.fori_loop(begin, end, body, 0)

    sweep(k_own, v_own, core, shard_chip)
    sweep(k_sib, v_sib, 1 - core, shard_chip + core)
    o_ref[...] = jnp.transpose(acc_ref[...] / l_ref[...]).astype(BF16)


def attention(info, qs, kvs, sibs, num_docs, tok, width):
    heads = width // HEAD_DIM
    chips = qs[0].shape[0]
    n_slab = len(qs)
    q_specs = [pl.BlockSpec((1, a.shape[1], HEAD_DIM), lambda h, s: (s[0], 0, h)) for a in qs]
    k_specs = [pl.BlockSpec((chips, a.shape[1], HEAD_DIM), lambda h, s: (0, 0, h)) for a in kvs]
    v_specs = [pl.BlockSpec((chips, a.shape[1], HEAD_DIM), lambda h, s: (0, 0, heads + h)) for a in kvs]
    grid_spec = pltpu.PrefetchScalarGridSpec(
        num_scalar_prefetch=1,
        grid=(heads,),
        in_specs=q_specs + k_specs + v_specs + k_specs + v_specs,
        out_specs=pl.BlockSpec((tok, HEAD_DIM), lambda h, s: (0, h)),
        scratch_shapes=[pltpu.VMEM((1, tok), F32), pltpu.VMEM((1, tok), F32), pltpu.VMEM((HEAD_DIM, tok), F32)],
    )
    return pl.pallas_call(
        functools.partial(attn_kernel, num_docs, n_slab),
        grid_spec=grid_spec,
        out_shape=jax.ShapeDtypeStruct((tok, width), BF16),
        compiler_params=params(),
        cost_estimate=cost(2 * 2 * tok * 5 * tok * width, 4 * chips * tok * 2 * width),
        name="attend",
    )(info, *qs, *kvs, *kvs, *sibs, *sibs)


def oproj_kernel(order, info_ref, *refs):
    chips = len(order)
    o_refs = refs[:chips]
    h_ref, g_ref, w_ref, h1_ref, b_ref, w_buf, sems = refs[chips:]
    width = w_buf.shape[1]

    def copy(i):
        src = lax.rem(info_ref[0] + chips - order[i], chips)
        return pltpu.make_async_copy(w_ref.at[pl.ds(pl.multiple_of(src * width, width), width), :], w_buf.at[i], sems.at[i])

    for i in range(chips):
        copy(i).start()
    acc = h_ref[...].astype(F32)
    total = None
    for i in range(chips):
        copy(i).wait()
        part = dot32(o_refs[i][...], w_buf[i])
        total = part if total is None else total + part
    h1 = (acc + total).astype(BF16)
    h1_ref[...] = h1
    wide = h1.astype(F32)
    b_ref[...] = (wide * lax.rsqrt(jnp.mean(wide * wide, axis=-1, keepdims=True) + NORM_EPS) * g_ref[...].astype(F32)).astype(BF16)


def oproj(info, outs, order, h_zero, norm, w_o):
    tok, hid = h_zero.shape
    width = outs[0].shape[1]
    chips = len(outs)
    vm = pl.BlockSpec(memory_space=pltpu.VMEM)
    return pl.pallas_call(
        functools.partial(oproj_kernel, order),
        in_specs=[pl.BlockSpec(memory_space=pltpu.SMEM)] + [vm] * (chips + 2) + [pl.BlockSpec(memory_space=pl.ANY)],
        out_specs=[vm, vm],
        out_shape=[jax.ShapeDtypeStruct((tok, hid), BF16)] * 2,
        scratch_shapes=[pltpu.VMEM((chips, width, hid), BF16), pltpu.SemaphoreType.DMA((chips,))],
        compiler_params=params(),
        cost_estimate=cost(2 * tok * hid * chips * width, 2 * chips * width * hid),
        name="oproj",
    )(info, *outs, h_zero, norm[None], w_o)


def mlp_kernel(h_ref, b_ref, wg_ref, wu_ref, wd_ref, out_ref, acc_ref):
    step = pl.program_id(0)

    @pl.when(step == 0)
    def _():
        acc_ref[...] = h_ref[...].astype(F32)

    b = b_ref[...]
    gate = dot32(b, wg_ref[...])
    up = dot32(b, wu_ref[...])
    act = (jax.nn.silu(gate) * up).astype(BF16)
    acc_ref[...] += dot32(act, wd_ref[...])

    @pl.when(step == pl.num_programs(0) - 1)
    def _():
        out_ref[...] = acc_ref[...].astype(BF16)


def mlp(h_one, normed, w_gate, w_up, w_down):
    tok, hid = h_one.shape
    ffn = w_gate.shape[1]
    tile = 768
    whole = lambda i: (0, 0)
    return pl.pallas_call(
        mlp_kernel,
        grid=(ffn // tile,),
        in_specs=[
            pl.BlockSpec((tok, hid), whole),
            pl.BlockSpec((tok, hid), whole),
            pl.BlockSpec((hid, tile), lambda i: (0, i)),
            pl.BlockSpec((hid, tile), lambda i: (0, i)),
            pl.BlockSpec((tile, hid), lambda i: (i, 0)),
        ],
        out_specs=pl.BlockSpec((tok, hid), whole),
        out_shape=jax.ShapeDtypeStruct((tok, hid), BF16),
        scratch_shapes=[pltpu.VMEM((tok, hid), F32)],
        compiler_params=params(),
        cost_estimate=cost(6 * tok * hid * ffn, 6 * hid * ffn),
        name="mlp",
    )(h_one, normed, w_gate, w_up, w_down)


def rope_tables(rope_pos):
    half = HEAD_DIM // 2
    inv_freq = ROPE_THETA ** (-jnp.arange(0, HEAD_DIM, 2, dtype=F32) / HEAD_DIM)
    idx = jnp.arange(half)
    lo, hi = MROPE_SPLIT
    chosen = jnp.where(idx < lo, rope_pos[:, 0, :, None], jnp.where(idx < hi, rope_pos[:, 1, :, None], rope_pos[:, 2, :, None]))
    angles = chosen.astype(F32) * inv_freq
    cos_h, sin_h = jnp.cos(angles), jnp.sin(angles)
    return jnp.concatenate([cos_h, cos_h], axis=-1), jnp.concatenate([-sin_h, sin_h], axis=-1)


def solution(mesh):
    group = mesh.shape['sp']
    chips = group // CORES
    row_spec = P(('dp', 'sp'), None)
    same_core = [[CORES * j + c for j in range(chips)] for c in range(CORES)]
    sibling = [(i, CORES * (i // CORES) + (i + 1) % CORES) for i in range(group)]

    def local_step(patches, embeds, dest_slot, rope_pos, cu_doc, ln_w, ln_b, w_one, b_one, w_two, b_two, norm_attn, w_q, b_q, w_k, b_k, w_v, b_v, w_o, norm_mlp, w_gate, w_up, w_down):
        tok, hid = embeds.shape
        merged_dev = dest_slot.shape[0]
        num_docs = cu_doc.shape[0] - 1
        me = lax.axis_index('sp')
        chip, core = me // CORES, me % CORES
        width = w_q.shape[1] // chips

        ints = jnp.concatenate([rope_pos, jnp.pad(dest_slot, (0, tok - merged_dev))[None]], axis=0)
        ints_all = lax.all_gather(ints, 'sp')
        slots = ints_all[:, 3, :merged_dev].reshape(-1)
        pos_own = lax.dynamic_index_in_dim(ints_all.reshape(chips, CORES, 4, tok), core, 1, keepdims=False)[:, :3]
        cos_t, sin_t = rope_tables(pos_own)

        cuts = ((0, tok // 2), (tok // 2, 3 * tok // 4), (3 * tok // 4, tok))
        gathered = []
        merged = None
        for n, (r0, r1) in enumerate(cuts):
            gathered.append(lax.all_gather(embeds[r0:r1], 'sp', axis_index_groups=same_core))
            if n == 0:
                merged = merger(patches, ln_w, ln_b, w_one, b_one, w_two, b_two)
                m_all = lax.all_gather(merged, 'sp', tiled=True)

        info = jnp.stack([chip, core, jnp.int32(tok)]).astype(jnp.int32)
        placed, mask = place(info, slots, m_all, chips, tok)
        h_zero = jnp.where(lax.dynamic_index_in_dim(mask, chip, 0, keepdims=False)[:, :1] > 0.5,
                           lax.dynamic_index_in_dim(placed, chip, 0, keepdims=False), embeds)

        qs, kvs, sibs = [], [], []
        for (r0, r1), e in zip(cuts, gathered):
            q, kv = qkv(info, e, placed, mask, cos_t, sin_t, norm_attn, w_q, b_q, w_k, b_k, w_v, b_v, r0, width)
            qs.append(q)
            kvs.append(kv)
            sibs.append(lax.ppermute(kv, 'sp', sibling))

        order = sorted(range(chips), key=lambda s: -min(s, chips - s))
        outs = []
        for s in order:
            target = (chip + s) % chips
            att_info = jnp.concatenate([jnp.stack([target, core]), cu_doc]).astype(jnp.int32)
            o = attention(att_info, qs, kvs, sibs, num_docs, tok, width)
            if s:
                o = lax.ppermute(o, 'sp', [(i, (i + CORES * s) % group) for i in range(group)])
            outs.append(o)
        h_one, normed = oproj(info, outs, tuple(order), h_zero, norm_mlp, w_o)
        return mlp(h_one, normed, w_gate, w_up, w_down)

    in_specs = (row_spec, row_spec, P(('dp', 'sp')), P(None, ('dp', 'sp')), P('dp')) + (P(),) * 18
    return jax.shard_map(local_step, mesh=mesh, in_specs=in_specs, out_specs=row_spec, check_vma=False)
```

time: 643 us -> 491 us (0.76)
  the two profiles are of different devices: /device:TPU:113 before, /device:TPU:123 now
where the time goes in v1:
time: 491 us; the launch traced here: 486 us
  Pallas kernels  321 us (65%)
  waiting for transfers between devices  66.7 us (14%)
  starting transfers between devices  35.9 us (7%)
  blocking collectives  18.3 us (4%)
  other arithmetic  16.9 us (3%)
  local copies, waits for them, and re-layouts  14.3 us (3%)
  between operations  13.7 us (3%)
    pallas_call x4, Pallas kernels, attention(): pl.pallas_call(functools.partial(attn_kernel, num_docs, n_slab), grid_spe...  116 us
    pallas_call x1, Pallas kernels, mlp(): pl.pallas_call(mlp_kernel, grid=(ffn // tile,), in_specs=[pl.BlockSpec((t...  66 us
    pallas_call x3, Pallas kernels, qkv(): pl.pallas_call(qkv_kernel, grid_spec=grid_spec, out_shape=[jax.ShapeDtype...  55.4 us
    all_gather x3, waiting for transfers between devices, local_step(): lax.all_gather(embeds[r0:r1], 'sp', axis_index_groups=same_core)  46.5 us
    pallas_call x1, Pallas kernels, merger(): pl.pallas_call(merger_kernel, grid=(mid // tile,), in_specs=[pl.BlockSpec...  36 us
    ppermute x3, starting transfers between devices, local_step(): lax.ppermute(o, 'sp', [(i, (i + CORES * s) % group) for i in range(group)])  32.7 us
    pallas_call x1, Pallas kernels, place(): pl.pallas_call(place_kernel, grid_spec=grid_spec, out_shape=[jax.ShapeDty...  30 us
    all_gather x1, waiting for transfers between devices, local_step(): m_all = lax.all_gather(merged, 'sp', tiled=True)  19.5 us
  transfers between devices with their start and end apart: 10, of which 4 were waited for; matrix products, arithmetic and copies ran while one was open for 5% of the time, Pallas kernels for 32%

profile of v1, /device:TPU:123, one launch (start us, length us, event | category | flops | bytes accessed | tf_op | source)
XLA Modules:
  0.0 486.4 jit_solution(11166585482867134623)
XLA Ops:
  6.6 1.3 broadcast_in_dim.88.lnw_ref
  7.8 1.3 broadcast_in_dim.89.lnb_ref
  9.1 1.3 broadcast_in_dim.90.b1_ref
  10.4 1.3 broadcast_in_dim.91.b2_ref
  11.7 36.0 %merger.1 = bf16[256,2560]{1,0:T(8,128)(2,1)} custom-call(bf16[1024,1280]{1,0:T(8,128)(2,1)} %x_ref.1, bf16[1,1280]{1,0:T(2,128)(2,1)} %broadcast_in_dim.88.lnw_ref, bf16[1,1280]{1,0:T(2,128)(2,1)} %broadcast_in_dim.89.lnb_ref, bf16[5120,5120]{1,0:T(8,128)(2,1)} %w1_ref.1, bf16[1,5120]{1,0:T(2,128)(2,1)} %broadcast_in_dim.90.b1_ref, ...), custom_call_target="tpu_custom_call" | custom-call | flops 20132659200 | bytes 78643200 | tf_op jit(solution)/shard_map/merger/pallas_call | solution.py:68
  47.8 1.1 slice.28
  49.1 1.1 fusion.3
  51.1 18.3 %all-gather.4 = s32[8,4,512]{2,1,0:T(4,128)S(1)} all-gather(s32[1,4,512]{2,1,0:T(4,128)S(1)} %add_bitcast_fusion), channel_id=3, replica_groups=mesh['dp'=2,'sp'=8] {'sp'}, dimensions={0}, use_global_device_ids=true | all-gather | bytes 73728 | tf_op jit(solution)/shard_map/all_gather | solution.py:422
  69.4 9.3 %fusion.2 = (f32[4,512,64]{2,1,0:T(8,128)S(1)}, f32[4,512,64]{2,1,0:T(8,128)S(1)}, f32[4,512,64]{2,1,0:T(8,128)S(1)}) fusion(f32[64]{0:T(128)S(1)} %multiply_power_fusion, s32[4,512]{1,0:T(4,128)S(1)} %get-tuple-element.28, s32[4,512]{1,0:T(4,128)S(1)} %get-tuple-element.29, pred[64]{0:T(512)(128)(4,1)S(1)} %iota_compare_fusion, ...), kind=kLoop, calls=%fused_computation.8 | loop fusion | flops 655360 | bytes 1597824 | tf_op jit(solution)/shard_map/neg | solution.py:403
  78.8 1.9 pad_maximum_fusion
  84.4 19.5 %all-gather.10.cloned.1.call-done.m_ref = bf16[2048,2560]{1,0:T(8,128)(2,1)} async-done(((bf16[256,2560]{1,0:T(8,128)(2,1)}), bf16[2048,2560]{1,0:T(8,128)(2,1)}) %all-gather.10.cloned.1.call-update) | async-done | bytes 10485776 | tf_op jit(solution)/shard_map/all_gather | solution.py:434
  103.9 30.0 %place.1 = (bf16[4,512,2560]{2,1,0:T(8,128)(2,1)}, bf16[4,512,128]{2,1,0:T(8,128)(2,1)}) custom-call(s32[3]{0:T(128)} %pad_add_fusion.info_ref, s32[1,2048]{1,0:T(1,128)} %bitcast.33, bf16[2048,2560]{1,0:T(8,128)(2,1)} %all-gather.10.cloned.1.call-done.m_ref), custom_call_target="tpu_custom_call" | custom-call | flops 21474836480 | bytes 20971520 | tf_op jit(solution)/shard_map/place/pallas_call | solution.py:121
  133.9 24.2 %all-gather.12.cloned.1.call-done = bf16[1024,2560]{1,0:T(8,128)(2,1)} async-done(((bf16[256,2560]{1,0:T(8,128)(2,1)}), bf16[1024,2560]{1,0:T(8,128)(2,1)}) %all-gather.12.cloned.1.call-update) | async-done | bytes 5242896 | tf_op jit(solution)/shard_map/all_gather | solution.py:431
  158.1 26.1 %qkv.3 = (bf16[4,256,640]{2,1,0:T(8,128)(2,1)}, bf16[4,256,1280]{2,1,0:T(8,128)(2,1)}) custom-call(s32[3]{0:T(128)} %pad_add_fusion.info_ref, bf16[4,256,2560]{2,1,0:T(8,128)(2,1)} %bitcast.27, bf16[4,512,2560]{2,1,0:T(8,128)(2,1)} %get-tuple-element.15.p_ref, bf16[4,512,128]{2,1,0:T(8,128)(2,1)} %get-tuple-element.16.mask_ref, ...), custom_call_target="tpu_custom_call" | custom-call | flops 10066329600 | bytes 20316160 | tf_op jit(solution)/shard_map/qkv/pallas_call | solution.py:203
  184.2 1.0 collective-permute-start
  185.2 5.4 %all-gather.14.cloned.1.call-done = bf16[512,2560]{1,0:T(8,128)(2,1)} async-done(((bf16[128,2560]{1,0:T(8,128)(2,1)}), bf16[512,2560]{1,0:T(8,128)(2,1)}) %all-gather.14.cloned.1.call-update) | async-done | bytes 2621456 | tf_op jit(solution)/shard_map/all_gather | solution.py:431
  190.6 14.5 %qkv.4 = (bf16[4,128,640]{2,1,0:T(8,128)(2,1)}, bf16[4,128,1280]{2,1,0:T(8,128)(2,1)}) custom-call(s32[3]{0:T(128)} %pad_add_fusion.info_ref, bf16[4,128,2560]{2,1,0:T(8,128)(2,1)} %bitcast.29, bf16[4,512,2560]{2,1,0:T(8,128)(2,1)} %get-tuple-element.15.p_ref, bf16[4,512,128]{2,1,0:T(8,128)(2,1)} %get-tuple-element.16.mask_ref, ...), custom_call_target="tpu_custom_call" | custom-call | flops 5033164800 | bytes 15073280 | tf_op jit(solution)/shard_map/qkv/pallas_call | solution.py:203
  205.1 1.0 collective-permute-start.1
  206.1 16.9 %all-gather.16.cloned.1.call-done = bf16[512,2560]{1,0:T(8,128)(2,1)} async-done(((bf16[128,2560]{1,0:T(8,128)(2,1)}), bf16[512,2560]{1,0:T(8,128)(2,1)}) %all-gather.16.cloned.1.call-update) | async-done | bytes 2621456 | tf_op jit(solution)/shard_map/all_gather | solution.py:431
  223.0 14.8 %qkv.5 = (bf16[4,128,640]{2,1,0:T(8,128)(2,1)}, bf16[4,128,1280]{2,1,0:T(8,128)(2,1)}) custom-call(s32[3]{0:T(128)} %pad_add_fusion.info_ref, bf16[4,128,2560]{2,1,0:T(8,128)(2,1)} %bitcast.28, bf16[4,512,2560]{2,1,0:T(8,128)(2,1)} %get-tuple-element.15.p_ref, bf16[4,512,128]{2,1,0:T(8,128)(2,1)} %get-tuple-element.16.mask_ref, ...), custom_call_target="tpu_custom_call" | custom-call | flops 5033164800 | bytes 15073280 | tf_op jit(solution)/shard_map/qkv/pallas_call | solution.py:203
  237.8 1.0 collective-permute-start.2
  240.6 0.9 dynamic-slice_bitcast_fusion
  241.7 1.5 copy-done
  243.2 44.7 %attend.4 = bf16[512,640]{1,0:T(8,128)(2,1)} custom-call(s32[5]{0:T(128)} %add_add_fusion.refs_0_, bf16[4,256,640]{2,1,0:T(8,128)(2,1)} %get-tuple-element.17.refs_1_, bf16[4,128,640]{2,1,0:T(8,128)(2,1)} %get-tuple-element.18.refs_2_, bf16[4,128,640]{2,1,0:T(8,128)(2,1)} %get-tuple-element.19.refs_3_, ...), custom_call_target="tpu_custom_call" | custom-call | flops 3355443200 | bytes 10485760 | tf_op jit(solution)/shard_map/attend/pallas_call | solution.py:302
  288.0 33.8 %attend.5 = bf16[512,640]{1,0:T(8,128)(2,1)} custom-call(s32[5]{0:T(128)} %get-tuple-element.34.refs_0_, bf16[4,256,640]{2,1,0:T(8,128)(2,1)} %get-tuple-element.17.refs_1_, bf16[4,128,640]{2,1,0:T(8,128)(2,1)} %get-tuple-element.18.refs_2_, bf16[4,128,640]{2,1,0:T(8,128)(2,1)} %get-tuple-element.19.refs_3_, ...), custom_call_target="tpu_custom_call" | custom-call | flops 3355443200 | bytes 10485760 | tf_op jit(solution)/shard_map/attend/pallas_call | solution.py:302
  321.8 2.2 collective-permute-start.4
  324.0 14.1 %attend.6 = bf16[512,640]{1,0:T(8,128)(2,1)} custom-call(s32[5]{0:T(128)} %get-tuple-element.35.refs_0_, bf16[4,256,640]{2,1,0:T(8,128)(2,1)} %get-tuple-element.17.refs_1_, bf16[4,128,640]{2,1,0:T(8,128)(2,1)} %get-tuple-element.18.refs_2_, bf16[4,128,640]{2,1,0:T(8,128)(2,1)} %get-tuple-element.19.refs_3_, ...), custom_call_target="tpu_custom_call" | custom-call | flops 3355443200 | bytes 10485760 | tf_op jit(solution)/shard_map/attend/pallas_call | solution.py:302
  338.2 30.4 %collective-permute-start.5 = (bf16[512,640]{1,0:T(8,128)(2,1)}, bf16[512,640]{1,0:T(8,128)(2,1)}, u32[]{:S(2)}, u32[]{:S(2)}) collective-permute-start(bf16[512,640]{1,0:T(8,128)(2,1)} %attend.6), channel_id=1, source_target_pairs={{0,6},{1,7},{2,0},{3,1},{4,2},{5,3},{6,4},{7,5},{8,14},{9,15},{10,... | collective-permute-start | bytes 1966088 | tf_op jit(solution)/shard_map/ppermute | solution.py:455
  368.6 3.6 bitcast_select_fusion.refs_4_
  372.2 23.8 %attend.7.refs_3_ = bf16[512,640]{1,0:T(8,128)(2,1)} custom-call(s32[5]{0:T(128)} %get-tuple-element.33.refs_0_, bf16[4,256,640]{2,1,0:T(8,128)(2,1)} %get-tuple-element.17.refs_1_, bf16[4,128,640]{2,1,0:T(8,128)(2,1)} %get-tuple-element.18.refs_2_, bf16[4,128,640]{2,1,0:T(8,128)(2,1)} %get-tuple-element.19.refs_3_, ...), custom_call_target="tpu_custom_call" | custom-call | flops 3355443200 | bytes 10485760 | tf_op jit(solution)/shard_map/attend/pallas_call | solution.py:302
  396.9 16.7 %oproj.1 = (bf16[512,2560]{1,0:T(8,128)(2,1)}, bf16[512,2560]{1,0:T(8,128)(2,1)}) custom-call(s32[3]{0:T(128)} %pad_add_fusion.info_ref, bf16[512,640]{1,0:T(8,128)(2,1)} %copy-done.11, bf16[512,640]{1,0:T(8,128)(2,1)} %collective-permute-done.4.refs_1_, bf16[512,640]{1,0:T(8,128)(2,1)} %collective-permute-done.5.refs_2_, bf16[512,640]{1,0:T(8,128)(2,1)} %attend.7.refs_3_, ...), custom_call_target="tpu_custom_call" | custom-call | flops 6710886400 | bytes 13107200 | tf_op jit(solution)/shard_map/oproj/pallas_call | solution.py:341
  413.6 66.0 %mlp.1 = bf16[512,2560]{1,0:T(8,128)(2,1)} custom-call(bf16[512,2560]{1,0:T(8,128)(2,1)} %get-tuple-element.23.h_ref, bf16[512,2560]{1,0:T(8,128)(2,1)} %get-tuple-element.24.b_ref, bf16[2560,6912]{1,0:T(8,128)(2,1)} %wg_ref.1, bf16[2560,6912]{1,0:T(8,128)(2,1)} %wu_ref.1, bf16[6912,2560]{1,0:T(8,128)(2,1)} %wd_ref.1), custom_call_target="tpu_custom_call" | custom-call | flops 54358179840 | bytes 106168320 | tf_op jit(solution)/shard_map/mlp/pallas_call | solution.py:376
  (56 shorter events, 7.6 us)
Async XLA Ops:
  6.5 97.3 %all-gather.10.cloned.1.call-start = ((), (), s32[]{:S(2)}) async-start(), calls=%async_computation | async-start | bytes 11796480 | tf_op jit(solution)/shard_map/all_gather | solution.py:434
  11.7 36.1 %copy-start.1 = (bf16[512,2560]{1,0:T(8,128)(2,1)S(1)}, bf16[512,2560]{1,0:T(8,128)(2,1)}, u32[]{:S(2)}) copy-start(bf16[512,2560]{1,0:T(8,128)(2,1)} %param.24) | copy-start | bytes 7864324
  47.8 110.3 %all-gather.12.cloned.1.call-start = ((), (), s32[]{:S(2)}) async-start(), calls=%async_computation.1 | async-start | bytes 6553600 | tf_op jit(solution)/shard_map/all_gather | solution.py:431
  49.0 2.0 copy-start.10
  49.0 2.1 copy-start.3
  49.1 141.6 %all-gather.14.cloned.1.call-start = ((), (), s32[]{:S(2)}) async-start(), calls=%async_computation.2 | async-start | bytes 3276800 | tf_op jit(solution)/shard_map/all_gather | solution.py:431
  50.3 172.6 %all-gather.16.cloned.1.call-start = ((), (), s32[]{:S(2)}) async-start(), calls=%async_computation.3 | async-start | bytes 3276800 | tf_op jit(solution)/shard_map/all_gather | solution.py:431
  78.7 2.6 copy-start.4
  78.7 3.2 copy-start.5
  78.7 3.8 copy-start.6
  78.7 4.4 copy-start.7
  184.2 57.5 %collective-permute-start = (bf16[4,256,1280]{2,1,0:T(8,128)(2,1)}, bf16[4,256,1280]{2,1,0:T(8,128)(2,1)S(1)}, u32[]{:S(2)}, u32[]{:S(2)}) collective-permute-start(bf16[4,256,1280]{2,1,0:T(8,128)(2,1)} %get-tuple-element.20.refs_4_.refs_7_), channel_id=1, source_target_pairs={{0,1},{1,0},{2,3},{3,2},{4,5},{5,4},{6,7},{7,6},{8,9},{9,8},{10,11... | collective-permute-start | bytes 7864328 | tf_op jit(solution)/shard_map/ppermute | solution.py:446
  205.1 36.5 %collective-permute-start.1 = (bf16[4,128,1280]{2,1,0:T(8,128)(2,1)}, bf16[4,128,1280]{2,1,0:T(8,128)(2,1)}, u32[]{:S(2)}, u32[]{:S(2)}) collective-permute-start(bf16[4,128,1280]{2,1,0:T(8,128)(2,1)} %get-tuple-element.21.refs_5_.refs_8_), channel_id=1, source_target_pairs={{0,1},{1,0},{2,3},{3,2},{4,5},{5,4},{6,7},{7,6},{8,9},{9,8},{10,11... | collective-permute-start | bytes 3932168 | tf_op jit(solution)/shard_map/ppermute | solution.py:446
  223.0 15.8 %copy-start.8 = (bf16[2560]{0:T(1024)(128)(2,1)S(1)}, bf16[2560]{0:T(1024)(128)(2,1)}, u32[]{:S(2)}) copy-start(bf16[2560]{0:T(1024)(128)(2,1)} %param.42) | copy-start | bytes 15364
  223.0 16.4 %copy-start.9 = (s32[3]{0:T(128)S(1)}, s32[3]{0:T(128)}, u32[]{:S(2)}) copy-start(s32[3]{0:T(128)} %param.27) | copy-start | bytes 40
  237.8 3.9 collective-permute-start.2
  241.7 1.5 copy-start
  287.9 108.1 %collective-permute-start.3 = (bf16[512,640]{1,0:T(8,128)(2,1)}, bf16[512,640]{1,0:T(8,128)(2,1)S(1)}, u32[]{:S(2)}, u32[]{:S(2)}) collective-permute-start(bf16[512,640]{1,0:T(8,128)(2,1)} %attend.4), channel_id=1, source_target_pairs={{0,4},{1,5},{2,6},{3,7},{4,0},{5,1},{6,2},{7,3},{8,12},{9,13},{10,... | collective-permute-start | bytes 1966088 | tf_op jit(solution)/shard_map/ppermute | solution.py:455
  321.8 74.2 %collective-permute-start.4 = (bf16[512,640]{1,0:T(8,128)(2,1)}, bf16[512,640]{1,0:T(8,128)(2,1)}, u32[]{:S(2)}, u32[]{:S(2)}) collective-permute-start(bf16[512,640]{1,0:T(8,128)(2,1)} %attend.5), channel_id=1, source_target_pairs={{0,2},{1,3},{2,4},{3,5},{4,6},{5,7},{6,0},{7,1},{8,10},{9,11},{10,... | collective-permute-start | bytes 1966088 | tf_op jit(solution)/shard_map/ppermute | solution.py:455
  324.0 44.5 %copy-start.2 = (bf16[512,2560]{1,0:T(8,128)(2,1)S(1)}, bf16[512,2560]{1,0:T(8,128)(2,1)}, u32[]{:S(2)}) copy-start(bf16[512,2560]{1,0:T(8,128)(2,1)} %param.24) | copy-start | bytes 7864324
  338.2 57.9 %collective-permute-start.5 = (bf16[512,640]{1,0:T(8,128)(2,1)}, bf16[512,640]{1,0:T(8,128)(2,1)}, u32[]{:S(2)}, u32[]{:S(2)}) collective-permute-start(bf16[512,640]{1,0:T(8,128)(2,1)} %attend.6), channel_id=1, source_target_pairs={{0,6},{1,7},{2,0},{3,1},{4,2},{5,3},{6,4},{7,5},{8,14},{9,15},{10,... | collective-permute-start | bytes 1966088 | tf_op jit(solution)/shard_map/ppermute | solution.py:455
  396.0 0.8 copy-start.11
Sparse Core Ops, SparseCore 0:
  47.9 55.9 all-gather.9
  105.4 52.6 all-gather.11
  159.6 30.9 all-gather.13
  192.0 30.9 all-gather.15

commit v2 on v1

v2 whole, which is shorter than its diff:
```python
import functools

import jax
import jax.numpy as jnp
from jax import lax
from jax.experimental import pallas as pl
from jax.experimental.pallas import tpu as pltpu
from jax.sharding import PartitionSpec as P


HEAD_DIM = 128
NORM_EPS = 1e-6
ROPE_THETA = 1000000.0
MROPE_SPLIT = (16, 40)
CORES = 2
NEG_BIG = -1e30
LOG2_E = 1.4426950408889634
F32 = jnp.float32
BF16 = jnp.bfloat16
VMEM_LIMIT = 60 * 1024 * 1024


def cost(flops, nbytes, trans=0):
    return pl.CostEstimate(flops=int(flops), bytes_accessed=int(nbytes), transcendentals=int(trans))


def params(limit=VMEM_LIMIT):
    return pltpu.CompilerParams(vmem_limit_bytes=limit)


def dot32(lhs, rhs):
    return jnp.dot(lhs, rhs, preferred_element_type=F32)


def merger_kernel(x_ref, lnw_ref, lnb_ref, w1_ref, b1_ref, w2_ref, b2_ref, out_ref, wide_ref, z_ref, acc_ref):
    step = pl.program_id(0)
    rows, feat = out_ref.shape[0], x_ref.shape[1]

    @pl.when(step == 0)
    def _():
        x = x_ref[...].astype(F32)
        cent = x - jnp.mean(x, axis=-1, keepdims=True)
        var = jnp.mean(cent * cent, axis=-1, keepdims=True)
        normed = cent * lax.rsqrt(var + NORM_EPS) * lnw_ref[...].astype(F32) + lnb_ref[...].astype(F32)
        for j in range(feat // 128):
            wide_ref[j] = normed[:, j * 128:(j + 1) * 128]
        for i in range(4):
            for j in range(feat // 128):
                col = i * feat + j * 128
                z_ref[:, col:col + 128] = wide_ref[j, pl.ds(i, rows, stride=4), :].astype(BF16)
        acc_ref[...] = jnp.zeros_like(acc_ref)

    pre = dot32(z_ref[...], w1_ref[...]) + b1_ref[...].astype(F32)
    inner = (0.5 * pre * (1.0 + lax.erf(pre * 2.0 ** -0.5))).astype(BF16)
    acc_ref[...] += dot32(inner, w2_ref[...])

    @pl.when(step == pl.num_programs(0) - 1)
    def _():
        out_ref[...] = (acc_ref[...] + b2_ref[...].astype(F32)).astype(BF16)


def merger(patches, ln_w, ln_b, w_one, b_one, w_two, b_two):
    total, feat = patches.shape
    rows = total // 4
    depth, mid = w_one.shape
    hid = w_two.shape[1]
    tile = 512
    whole = lambda i: (0, 0)
    return pl.pallas_call(
        merger_kernel,
        grid=(mid // tile,),
        in_specs=[
            pl.BlockSpec((total, feat), whole),
            pl.BlockSpec((1, feat), whole),
            pl.BlockSpec((1, feat), whole),
            pl.BlockSpec((depth, tile), lambda i: (0, i)),
            pl.BlockSpec((1, tile), lambda i: (0, i)),
            pl.BlockSpec((tile, hid), lambda i: (i, 0)),
            pl.BlockSpec((1, hid), whole),
        ],
        out_specs=pl.BlockSpec((rows, hid), whole),
        out_shape=jax.ShapeDtypeStruct((rows, hid), BF16),
        scratch_shapes=[
            pltpu.VMEM((feat // 128, total, 128), F32),
            pltpu.VMEM((rows, depth), BF16),
            pltpu.VMEM((rows, hid), F32),
        ],
        compiler_params=params(),
        cost_estimate=cost(2 * rows * mid * (depth + hid), 2 * mid * (depth + hid)),
        name="merger",
    )(patches, ln_w[None], ln_b[None], w_one, b_one[None], w_two, b_two[None])


def stack_delta(i, chips):
    return jnp.where(i == chips - 1, chips // 2, jnp.where(i == chips - 2, chips - 1, i))


def place_kernel(sizes, chips, tok, info_ref, slots_ref, *refs):
    n = len(sizes)
    m_refs = refs[:n]
    placed_ref, mask_ref, m_buf, sems = refs[n:]
    step = pl.program_id(0)
    rows = placed_ref.shape[1]
    per_shard = tok // rows
    starts = [sum(sizes[:i]) for i in range(n)]

    def copy(i):
        return pltpu.make_async_copy(m_refs[i], m_buf.at[pl.ds(starts[i], sizes[i]), :], sems.at[i])

    @pl.when(step == 0)
    def _():
        for i in range(n):
            copy(i).start()
        for i in range(n):
            copy(i).wait()

    chip = lax.rem(info_ref[0] + stack_delta(step // per_shard, chips), chips)
    base = tok * (CORES * chip + info_ref[1]) + rows * (step % per_shard)
    pos = base + lax.broadcasted_iota(jnp.int32, (rows, slots_ref.shape[1]), 0)
    hit = (slots_ref[...] == pos).astype(F32)
    placed_ref[0] = dot32(hit.astype(BF16), m_buf[...]).astype(BF16)
    any_hit = jnp.max(hit, axis=1, keepdims=True)
    mask_ref[0] = jnp.broadcast_to(any_hit, mask_ref.shape[1:]).astype(BF16)


def place(info, slots, parts, chips, tok):
    rows = 256
    hid = parts[0].shape[1]
    per = tok // rows
    sizes = tuple(a.shape[0] for a in parts)
    grid_spec = pltpu.PrefetchScalarGridSpec(
        num_scalar_prefetch=1,
        grid=(chips * per,),
        in_specs=[pl.BlockSpec((1, slots.shape[0]), lambda i, s: (0, 0))] + [pl.BlockSpec(memory_space=pl.ANY)] * len(parts),
        out_specs=[
            pl.BlockSpec((1, rows, hid), lambda i, s: (i // per, i % per, 0)),
            pl.BlockSpec((1, rows, 128), lambda i, s: (i // per, i % per, 0)),
        ],
        scratch_shapes=[pltpu.VMEM((sum(sizes), hid), BF16), pltpu.SemaphoreType.DMA((len(sizes),))],
    )
    return pl.pallas_call(
        functools.partial(place_kernel, sizes, chips, tok),
        grid_spec=grid_spec,
        out_shape=[jax.ShapeDtypeStruct((chips, tok, hid), BF16), jax.ShapeDtypeStruct((chips, tok, 128), BF16)],
        compiler_params=params(),
        cost_estimate=cost(2 * chips * tok * sum(sizes) * hid, 2 * sum(sizes) * hid + 2 * chips * tok * hid),
        name="place",
    )(info, slots[None], *parts)


def qkv_kernel(first, piece_rows, want_h, info_ref, g_ref, mask_ref, cos_ref, sin_ref, bq_ref, bk_ref, bv_ref, placed_ref, wq_ref, wk_ref, wv_ref, *refs):
    n = len(piece_rows)
    total = sum(len(r) for r in piece_rows)
    e_refs = refs[:total]
    outs = refs[total:total + 3 + want_h]
    q_ref, k_ref, v_ref = outs[:3]
    e_buf, p_buf, a_buf, wq_buf, wk_buf, wv_buf, e_sems, p_sems, w_sems = refs[total + 3 + want_h:]
    width = wq_buf.shape[1]
    col = pl.multiple_of(info_ref[0] * width, width)
    weights = ((wq_ref, wq_buf), (wk_ref, wk_buf), (wv_ref, wv_buf))

    def load_weight(i):
        src, dst = weights[i]
        return pltpu.make_async_copy(src.at[:, pl.ds(col, width)], dst, w_sems.at[i])

    def loads(i):
        at = sum(len(r) for r in piece_rows[:i])
        row = 0
        out = [pltpu.make_async_copy(placed_ref.at[first + i], p_buf.at[i % 2], p_sems.at[i % 2])]
        for j, rows in enumerate(piece_rows[i]):
            out.append(pltpu.make_async_copy(e_refs[at + j], e_buf.at[i % 2, pl.ds(row, rows), :], e_sems.at[i % 2, j]))
            row += rows
        return out

    def prologue(i):
        for c in loads(i):
            c.wait()
        hit = mask_ref[first + i][:, :1].astype(F32) > 0.5
        h = jnp.where(hit, p_buf[i % 2].astype(F32), e_buf[i % 2].astype(F32))
        if want_h and i == 0:
            outs[3][...] = h.astype(BF16)
        a_buf[i % 2] = (h * lax.rsqrt(jnp.mean(h * h, axis=-1, keepdims=True) + NORM_EPS) * g_ref[...].astype(F32)).astype(BF16)

    for c in loads(0):
        c.start()
    for i in range(3):
        load_weight(i).start()
    prologue(0)
    for i in range(n):
        if i + 1 < n:
            for c in loads(i + 1):
                c.start()
        a = a_buf[i % 2]
        cos_t, sin_t = cos_ref[first + i], sin_ref[first + i]
        for j, (bias, out_ref) in enumerate(((bq_ref, q_ref), (bk_ref, k_ref), (bv_ref, v_ref))):
            if i == 0:
                load_weight(j).wait()
            lin = dot32(a, weights[j][1][...]) + bias[...].astype(F32)
            for h in range(width // HEAD_DIM):
                cols = slice(h * HEAD_DIM, (h + 1) * HEAD_DIM)
                part = lin[:, cols]
                if j < 2:
                    out_ref[i, :, cols] = (part * cos_t + pltpu.roll(part, HEAD_DIM // 2, 1) * sin_t).astype(BF16)
                else:
                    out_ref[i, cols, :] = jnp.transpose(part).astype(BF16)
        if i + 1 < n:
            prologue(i + 1)


def qkv(info, first, pieces, placed, mask, cos_t, sin_t, norm, w_q, b_q, w_k, b_k, w_v, b_v, width, want_h):
    tok, hid = placed.shape[1:]
    n = len(pieces)
    rows = tuple(tuple(a.shape[0] for a in p) for p in pieces)
    flat = [a for p in pieces for a in p]
    whole2 = lambda i, s: (0, 0)
    whole3 = lambda i, s: (0, 0, 0)
    bias = pl.BlockSpec((1, width), lambda i, s: (0, s[0]))
    anyspec = pl.BlockSpec(memory_space=pl.ANY)
    out_shape = [jax.ShapeDtypeStruct((n, tok, width), BF16)] * 2 + [jax.ShapeDtypeStruct((n, width, tok), BF16)]
    out_specs = [pl.BlockSpec((n, tok, width), whole3)] * 2 + [pl.BlockSpec((n, width, tok), whole3)]
    if want_h:
        out_shape.append(jax.ShapeDtypeStruct((tok, hid), BF16))
        out_specs.append(pl.BlockSpec((tok, hid), whole2))
    most = max(len(r) for r in rows)
    grid_spec = pltpu.PrefetchScalarGridSpec(
        num_scalar_prefetch=1,
        grid=(1,),
        in_specs=[
            pl.BlockSpec((1, hid), whole2),
            pl.BlockSpec(mask.shape, whole3),
            pl.BlockSpec(cos_t.shape, whole3),
            pl.BlockSpec(sin_t.shape, whole3),
            bias, bias, bias,
        ] + [anyspec] * (4 + len(flat)),
        out_specs=out_specs,
        scratch_shapes=[
            pltpu.VMEM((2, tok, hid), BF16),
            pltpu.VMEM((2, tok, hid), BF16),
            pltpu.VMEM((2, tok, hid), BF16),
            pltpu.VMEM((hid, width), BF16),
            pltpu.VMEM((hid, width), BF16),
            pltpu.VMEM((hid, width), BF16),
            pltpu.SemaphoreType.DMA((2, most)),
            pltpu.SemaphoreType.DMA((2,)),
            pltpu.SemaphoreType.DMA((3,)),
        ],
    )
    return pl.pallas_call(
        functools.partial(qkv_kernel, first, rows, int(want_h)),
        grid_spec=grid_spec,
        out_shape=out_shape,
        compiler_params=params(),
        cost_estimate=cost(2 * n * tok * hid * 3 * width, 2 * hid * 3 * width + 4 * n * tok * hid),
        name="qkv",
    )(info, norm[None], mask, cos_t, sin_t, b_q[None], b_k[None], b_v[None], placed, w_q, w_k, w_v, *flat)


def attn_kernel(num_docs, chips, head0, info_ref, *refs):
    q_in, k_own_in, k_sib_in, v_own_in, v_sib_in = (refs[2 * g:2 * g + 2] for g in range(5))
    o_ref, q_buf, k_buf, v_buf, sems, m_ref, l_ref, acc_ref = refs[10:]
    head = pl.program_id(0)
    slot = lax.rem(head, 2)
    my_chip, core = info_ref[0], info_ref[1]
    tok = o_ref.shape[1]

    def copies(h, s):
        col = pl.multiple_of((head0 + h) * HEAD_DIM, HEAD_DIM)
        out = []
        lo = 0
        for g in range(2):
            n = q_in[g].shape[0]
            span = pl.ds(lo, n)
            lo += n
            cols = pl.ds(col, HEAD_DIM)
            out.append(pltpu.make_async_copy(q_in[g].at[:, :, cols], q_buf.at[s, span], sems.at[s, 5 * g]))
            out.append(pltpu.make_async_copy(k_own_in[g].at[:, :, cols], k_buf.at[s, 0, span], sems.at[s, 5 * g + 1]))
            out.append(pltpu.make_async_copy(k_sib_in[g].at[:, :, cols], k_buf.at[s, 1, span], sems.at[s, 5 * g + 2]))
            out.append(pltpu.make_async_copy(v_own_in[g].at[:, cols, :], v_buf.at[s, 0, span], sems.at[s, 5 * g + 3]))
            out.append(pltpu.make_async_copy(v_sib_in[g].at[:, cols, :], v_buf.at[s, 1, span], sems.at[s, 5 * g + 4]))
        return out

    @pl.when(head == 0)
    def _():
        for c in copies(0, 0):
            c.start()

    @pl.when(head + 1 < pl.num_programs(0))
    def _():
        for c in copies(head + 1, 1 - slot):
            c.start()

    for c in copies(head, slot):
        c.wait()

    def place_of(chip):
        delta = lax.rem(chip - my_chip + chips, chips)
        return jnp.where(delta == chips // 2, chips - 1, jnp.where(delta == chips - 1, chips - 2, delta))

    def doc_start(pos):
        start = jnp.zeros_like(pos)
        for d in range(1, num_docs):
            cut = info_ref[2 + d]
            start = jnp.where(pos >= cut, cut, start)
        return start

    factor = HEAD_DIM ** -0.5 * LOG2_E
    halves = 2
    half = tok // halves

    def queries(q_chip, carry):
        q_at = place_of(q_chip)
        q_base = tok * (CORES * q_chip + core)
        q = q_buf[slot, q_at]
        q_pos = q_base + lax.broadcasted_iota(jnp.int32, (1, tok), 1)
        starts = doc_start(q_pos)
        lo_start = doc_start(q_base)
        hi_start = doc_start(q_base + tok - 1)

        def block(j, masked, fresh):
            at = place_of(j)
            bases = (tok * (CORES * j + core), tok * (CORES * j + 1 - core))
            ks = [k_buf[slot, b, at] for b in range(2)]
            vs = jnp.concatenate([v_buf[slot, b, at] for b in range(2)], axis=1)
            scores = [[lax.dot_general(k, q[i * half:(i + 1) * half], (((1,), (1,)), ((), ())), preferred_element_type=F32) for k in ks] for i in range(halves)]
            for i in range(halves):
                lanes = slice(i * half, (i + 1) * half)
                pair = scores[i]
                if masked:
                    for b in range(2):
                        k_pos = bases[b] + lax.broadcasted_iota(jnp.int32, pair[b].shape, 0)
                        pair[b] = jnp.where((k_pos <= q_pos[:, lanes]) & (k_pos >= starts[:, lanes]), pair[b], NEG_BIG)
                top = jnp.maximum(jnp.max(pair[0], axis=0, keepdims=True), jnp.max(pair[1], axis=0, keepdims=True))
                if not fresh:
                    old = m_ref[:, lanes]
                    top = jnp.maximum(top, old)
                probs = [jnp.exp2((s - top) * factor) for s in pair]
                total = jnp.sum(probs[0], axis=0, keepdims=True) + jnp.sum(probs[1], axis=0, keepdims=True)
                out = dot32(vs, jnp.concatenate([p.astype(BF16) for p in probs], axis=0))
                if not fresh:
                    alpha = jnp.exp2((old - top) * factor)
                    total = total + l_ref[:, lanes] * alpha
                    out = out + acc_ref[:, lanes] * alpha
                m_ref[:, lanes] = top
                l_ref[:, lanes] = total
                acc_ref[:, lanes] = out

        block(q_chip, True, True)

        def body(t, inner):
            j = q_chip - 1 - t
            clear = tok * CORES * j >= hi_start

            @pl.when(clear)
            def _():
                block(j, False, False)

            @pl.when(jnp.logical_not(clear))
            def _():
                block(j, True, False)

            return inner

        lax.fori_loop(0, q_chip - lo_start // (tok * CORES), body, 0)
        o_ref[q_at] = jnp.transpose(acc_ref[...] / l_ref[...]).astype(BF16)
        return carry

    lax.fori_loop(0, chips, queries, 0)


def attention(info, qs, ks, k_sibs, vs, v_sibs, num_docs, chips, tok, head0, heads):
    grid_spec = pltpu.PrefetchScalarGridSpec(
        num_scalar_prefetch=1,
        grid=(heads,),
        in_specs=[pl.BlockSpec(memory_space=pl.ANY)] * 10,
        out_specs=pl.BlockSpec((chips, tok, HEAD_DIM), lambda h, s: (0, 0, h)),
        scratch_shapes=[
            pltpu.VMEM((2, chips, tok, HEAD_DIM), BF16),
            pltpu.VMEM((2, 2, chips, tok, HEAD_DIM), BF16),
            pltpu.VMEM((2, 2, chips, HEAD_DIM, tok), BF16),
            pltpu.SemaphoreType.DMA((2, 10)),
            pltpu.VMEM((1, tok), F32),
            pltpu.VMEM((1, tok), F32),
            pltpu.VMEM((HEAD_DIM, tok), F32),
        ],
    )
    width = heads * HEAD_DIM
    return pl.pallas_call(
        functools.partial(attn_kernel, num_docs, chips, head0),
        grid_spec=grid_spec,
        out_shape=jax.ShapeDtypeStruct((chips, tok, width), BF16),
        compiler_params=params(),
        cost_estimate=cost(2 * 2 * 20 * tok * tok * width, 2 * 5 * chips * tok * width),
        name="attend",
    )(info, *qs, *ks, *k_sibs, *vs, *v_sibs)


def oproj_kernel(shifts, info_ref, *refs):
    chips = len(shifts)
    n = 2 * chips
    o_refs = refs[:n]
    h_ref, g_ref, w_ref, h1_ref, b_ref, w_bufs, o_bufs, sems = refs[n], refs[n + 1], refs[n + 2], refs[n + 3], refs[n + 4], refs[n + 5:n + 7], refs[n + 7:n + 9], refs[n + 9]
    widths = [o_refs[0].shape[1], o_refs[chips].shape[1]]

    def copies(g, i):
        wide = widths[g]
        src = lax.rem(info_ref[0] + 2 * chips - shifts[i], chips)
        row = pl.multiple_of(src * sum(widths) + g * widths[0], HEAD_DIM)
        return (
            pltpu.make_async_copy(w_ref.at[pl.ds(row, wide), :], w_bufs[g].at[pl.ds(i * wide, wide), :], sems.at[g, i]),
            pltpu.make_async_copy(o_refs[g * chips + i], o_bufs[g].at[:, pl.ds(i * wide, wide)], sems.at[g, chips + i]),
        )

    for g in range(2):
        for i in range(chips):
            for c in copies(g, i):
                c.start()
    parts = []
    for g in range(2):
        for i in range(chips):
            for c in copies(g, i):
                c.wait()
        parts.append(dot32(o_bufs[g][...], w_bufs[g][...]))
    h1 = (h_ref[...].astype(F32) + (parts[0] + parts[1])).astype(BF16)
    h1_ref[...] = h1
    wide = h1.astype(F32)
    b_ref[...] = (wide * lax.rsqrt(jnp.mean(wide * wide, axis=-1, keepdims=True) + NORM_EPS) * g_ref[...].astype(F32)).astype(BF16)


def oproj(info, outs_a, outs_b, shifts, h_zero, norm, w_o):
    tok, hid = h_zero.shape
    wide_a, wide_b = outs_a[0].shape[1], outs_b[0].shape[1]
    chips = len(shifts)
    vm = pl.BlockSpec(memory_space=pltpu.VMEM)
    anyspec = pl.BlockSpec(memory_space=pl.ANY)
    return pl.pallas_call(
        functools.partial(oproj_kernel, shifts),
        in_specs=[pl.BlockSpec(memory_space=pltpu.SMEM)] + [anyspec] * (2 * chips) + [vm] * 2 + [anyspec],
        out_specs=[vm, vm],
        out_shape=[jax.ShapeDtypeStruct((tok, hid), BF16)] * 2,
        scratch_shapes=[
            pltpu.VMEM((chips * wide_a, hid), BF16),
            pltpu.VMEM((chips * wide_b, hid), BF16),
            pltpu.VMEM((tok, chips * wide_a), BF16),
            pltpu.VMEM((tok, chips * wide_b), BF16),
            pltpu.SemaphoreType.DMA((2, 2 * chips)),
        ],
        compiler_params=params(),
        cost_estimate=cost(2 * tok * hid * chips * (wide_a + wide_b), 2 * chips * (wide_a + wide_b) * hid),
        name="oproj",
    )(info, *outs_a, *outs_b, h_zero, norm[None], w_o)


def mlp_kernel(h_ref, b_ref, wg_ref, wu_ref, wd_ref, out_ref, acc_ref):
    step = pl.program_id(0)

    @pl.when(step == 0)
    def _():
        acc_ref[...] = h_ref[...].astype(F32)

    b = b_ref[...]
    gate = dot32(b, wg_ref[...])
    up = dot32(b, wu_ref[...])
    act = (jax.nn.silu(gate) * up).astype(BF16)
    acc_ref[...] += dot32(act, wd_ref[...])

    @pl.when(step == pl.num_programs(0) - 1)
    def _():
        out_ref[...] = acc_ref[...].astype(BF16)


def mlp(h_one, normed, w_gate, w_up, w_down):
    tok, hid = h_one.shape
    ffn = w_gate.shape[1]
    tile = 768
    whole = lambda i: (0, 0)
    return pl.pallas_call(
        mlp_kernel,
        grid=(ffn // tile,),
        in_specs=[
            pl.BlockSpec((tok, hid), whole),
            pl.BlockSpec((tok, hid), whole),
            pl.BlockSpec((hid, tile), lambda i: (0, i)),
            pl.BlockSpec((hid, tile), lambda i: (0, i)),
            pl.BlockSpec((tile, hid), lambda i: (i, 0)),
        ],
        out_specs=pl.BlockSpec((tok, hid), whole),
        out_shape=jax.ShapeDtypeStruct((tok, hid), BF16),
        scratch_shapes=[pltpu.VMEM((tok, hid), F32)],
        compiler_params=params(),
        cost_estimate=cost(6 * tok * hid * ffn, 6 * hid * ffn),
        name="mlp",
    )(h_one, normed, w_gate, w_up, w_down)


def rope_tables(rope_pos):
    half = HEAD_DIM // 2
    inv_freq = ROPE_THETA ** (-jnp.arange(0, HEAD_DIM, 2, dtype=F32) / HEAD_DIM)
    idx = jnp.arange(half)
    lo, hi = MROPE_SPLIT
    chosen = jnp.where(idx < lo, rope_pos[:, 0, :, None], jnp.where(idx < hi, rope_pos[:, 1, :, None], rope_pos[:, 2, :, None]))
    angles = chosen.astype(F32) * inv_freq
    cos_h, sin_h = jnp.cos(angles), jnp.sin(angles)
    return jnp.concatenate([cos_h, cos_h], axis=-1), jnp.concatenate([-sin_h, sin_h], axis=-1)


def solution(mesh):
    group = mesh.shape['sp']
    chips = group // CORES
    row_spec = P(('dp', 'sp'), None)
    sibling = [(i, CORES * (i // CORES) + (i + 1) % CORES) for i in range(group)]

    def hop(x, steps):
        return lax.ppermute(x, 'sp', [(i, (i + CORES * steps) % group) for i in range(group)])

    def swap(x):
        return lax.ppermute(x, 'sp', sibling)

    def step(patches, embeds, dest_slot, rope_pos, cu_doc, ln_w, ln_b, w_one, b_one, w_two, b_two, norm_attn, w_q, b_q, w_k, b_k, w_v, b_v, w_o, norm_mlp, w_gate, w_up, w_down):
        tok, _ = embeds.shape
        merged_dev = dest_slot.shape[0]
        num_docs = cu_doc.shape[0] - 1
        me = lax.axis_index('sp')
        chip, core = me // CORES, me % CORES
        width = w_q.shape[1] // chips
        mid = tok // 2
        quarter = mid // 2
        half_m = merged_dev // 2
        info = jnp.stack([chip, core]).astype(jnp.int32)

        ints = jnp.concatenate([rope_pos, jnp.pad(dest_slot, (0, tok - merged_dev))[None]], axis=0)
        ints_all = lax.all_gather(ints, 'sp').reshape(chips, CORES, 4, tok)
        rolled = lax.dynamic_slice_in_dim(jnp.concatenate([ints_all, ints_all], axis=0), chip, chips, 0)
        rolled = jnp.stack([rolled[0], rolled[1], rolled[3], rolled[2]])
        own = lax.dynamic_index_in_dim(rolled, core, 1, keepdims=False)
        sib = lax.dynamic_index_in_dim(rolled, 1 - core, 1, keepdims=False)
        slots = jnp.concatenate([own[:, 3, :merged_dev], sib[:, 3, :merged_dev]]).reshape(-1)
        cos_t, sin_t = rope_tables(own[:, :3])
        embeds, ints_all = lax.optimization_barrier((embeds, ints_all))

        e_a, e_b = embeds[:mid], embeds[mid:]
        a_prev = hop(e_a, 1)
        a_next = hop(e_a, -1)
        merged = merger(patches, ln_w, ln_b, w_one, b_one, w_two, b_two)
        m_prev = hop(merged, 1)
        m_next = hop(merged, -1)
        m_far_lo = hop(m_prev[:half_m], 1)
        m_far_hi = hop(m_next[half_m:], -1)
        mine = [merged, m_next, m_prev, m_far_lo, m_far_hi]
        theirs = [swap(m) for m in mine]
        b_prev = hop(e_b, 1)
        b_next = hop(e_b, -1)
        a_far_lo = hop(a_prev[:quarter], 1)
        a_far_hi = hop(a_next[quarter:], -1)
        b_far_lo = hop(b_prev[:quarter], 1)
        b_far_hi = hop(b_next[quarter:], -1)

        placed, mask = place(info, slots, mine + theirs, chips, tok)
        common = (placed, mask, cos_t, sin_t, norm_attn, w_q, b_q, w_k, b_k, w_v, b_v, width)
        near = [[embeds], [a_next, b_next], [a_prev, b_prev]]
        q_n, k_n, v_n, h_zero = qkv(info, 0, near, *common, True)
        far = [[a_far_lo, a_far_hi, b_far_lo, b_far_hi]]
        k_sib_n, v_sib_n = swap(k_n), swap(v_n)
        q_f, k_f, v_f = qkv(info, len(near), far, *common, False)
        k_sibs = [k_sib_n, swap(k_f)]
        v_sibs = [v_sib_n, swap(v_f)]

        att_info = jnp.concatenate([info, cu_doc]).astype(jnp.int32)
        heads = width // HEAD_DIM
        split = (heads + 1) // 2
        shifts = (0, 1, -1, chips // 2)
        parts = []
        for head0, n in ((0, split), (split, heads - split)):
            o = attention(att_info, (q_n, q_f), (k_n, k_f), k_sibs, (v_n, v_f), v_sibs, num_docs, chips, tok, head0, n)
            parts.append([o[0]] + [hop(o[i], shifts[i]) for i in range(1, chips)])
        h_one, normed = oproj(info, parts[0], parts[1], shifts, h_zero, norm_mlp, w_o)
        return mlp(h_one, normed, w_gate, w_up, w_down)

    in_specs = (row_spec, row_spec, P(('dp', 'sp')), P(None, ('dp', 'sp')), P('dp')) + (P(),) * 18
    return jax.shard_map(step, mesh=mesh, in_specs=in_specs, out_specs=row_spec, check_vma=False)
```

time: 491 us -> 491 us (level)
  the two profiles are of different devices: /device:TPU:123 before, /device:TPU:122 now
where the time goes in v2:
time: 491 us; the launch traced here: 487 us
  Pallas kernels  267 us (54%)
  waiting for transfers between devices  106 us (22%)
  blocking collectives  48 us (10%)
  local copies, waits for them, and re-layouts  27.5 us (6%)
  starting transfers between devices  24 us (5%)
  other arithmetic  13.3 us (3%)
    ppermute x18, waiting for transfers between devices, hop(): lax.ppermute(x, 'sp', [(i, (i + CORES * steps) % group) for i in range(gr...  104 us
    pallas_call x1, Pallas kernels, mlp(): pl.pallas_call(mlp_kernel, grid=(ffn // tile,), in_specs=[pl.BlockSpec((t...  65.9 us
    pallas_call x2, Pallas kernels, attention(): pl.pallas_call(functools.partial(attn_kernel, num_docs, chips, head0), gr...  65.6 us
    pallas_call x2, Pallas kernels, qkv(): pl.pallas_call(functools.partial(qkv_kernel, first, rows, int(want_h)), g...  52 us
    all_gather x1, blocking collectives, step(): ints_all = lax.all_gather(ints, 'sp').reshape(chips, CORES, 4, tok)  48 us
    pallas_call x1, Pallas kernels, merger(): pl.pallas_call(merger_kernel, grid=(mid // tile,), in_specs=[pl.BlockSpec...  35.9 us
    pallas_call x1, Pallas kernels, place(): pl.pallas_call(functools.partial(place_kernel, sizes, chips, tok), grid_s...  30.7 us
    ppermute x18, starting transfers between devices, hop(): lax.ppermute(x, 'sp', [(i, (i + CORES * steps) % group) for i in range(gr...  22 us
  transfers between devices with their start and end apart: 27, of which 9 were waited for; matrix products, arithmetic and copies ran while one was open for 5% of the time, Pallas kernels for 25%

profile of v2, /device:TPU:122, one launch (start us, length us, event | category | flops | bytes accessed | tf_op | source)
XLA Modules:
  0.0 486.7 jit_solution(2265754304914160605)
XLA Ops:
  2.6 1.3 broadcast_in_dim.77.b1_ref
  5.2 35.9 %merger.1.refs_0_ = bf16[256,2560]{1,0:T(8,128)(2,1)} custom-call(bf16[1024,1280]{1,0:T(8,128)(2,1)} %x_ref.1, bf16[1,1280]{1,0:T(2,128)(2,1)} %broadcast_in_dim.75.lnw_ref, bf16[1,1280]{1,0:T(2,128)(2,1)} %broadcast_in_dim.76.lnb_ref, bf16[5120,5120]{1,0:T(8,128)(2,1)} %w1_ref.1, bf16[1,5120]{1,0:T(2,128)(2,1)} %broadcast_in_dim.77.b1_ref, ...), custom_call_target="tpu_custom_call" | custom-call | flops 20132659200 | bytes 78643200 | tf_op jit(solution)/shard_map/merger/pallas_call | solution.py:69
  41.5 1.6 collective-permute-start.1
  43.2 48.0 %all-gather.1 = s32[8,4,512]{2,1,0:T(4,128)S(1)} all-gather(s32[1,4,512]{2,1,0:T(4,128)S(1)} %add_bitcast_fusion), channel_id=2, replica_groups=mesh['dp'=2,'sp'=8] {'sp'}, dimensions={0}, use_global_device_ids=true | all-gather | bytes 73728 | tf_op jit(solution)/shard_map/all_gather | solution.py:531
  91.2 1.7 fusion.4
  94.5 2.5 collective-permute-start.2
  98.6 26.3 %collective-permute-done.11.refs_3_ = bf16[256,2560]{1,0:T(8,128)(2,1)S(1)} collective-permute-done((bf16[256,2560]{1,0:T(8,128)(2,1)}, bf16[256,2560]{1,0:T(8,128)(2,1)S(1)}, u32[]{:S(2)}, u32[]{:S(2)}) %collective-permute-start.11) | collective-permute-done | bytes 1310752 | tf_op jit(solution)/shard_map/ppermute | solution.py:513
  128.1 4.9 collective-permute-done.2.refs_3_
  134.1 9.3 %fusion.2 = (f32[4,512,64]{2,1,0:T(8,128)S(1)}, f32[4,512,64]{2,1,0:T(8,128)S(1)}, f32[4,512,64]{2,1,0:T(8,128)S(1)}) fusion(f32[64]{0:T(128)S(1)} %multiply_power_fusion, s32[4,512]{1,0:T(4,128)S(1)} %get-tuple-element.44, s32[4,512]{1,0:T(4,128)S(1)} %get-tuple-element.45, pred[64]{0:T(512)(128)(4,1)S(1)} %get-tuple-element.51, ...), kind=kLoop, calls=%fused_computation.15 | loop fusion | flops 655360 | bytes 1597824 | tf_op jit(solution)/shard_map/neg | solution.py:503
  143.4 1.3 pad_maximum_fusion.cos_ref
  144.7 1.4 pad_maximum_fusion.1.sin_ref
  148.2 1.7 collective-permute-start.10
  153.1 30.7 %place.1 = (bf16[4,512,2560]{2,1,0:T(8,128)(2,1)}, bf16[4,512,128]{2,1,0:T(8,128)(2,1)}) custom-call(s32[2]{0:T(128)} %pad_add_fusion.1.info_ref, s32[1,2048]{1,0:T(1,128)} %bitcast.42, bf16[256,2560]{1,0:T(8,128)(2,1)} %merger.1.refs_0_, bf16[256,2560]{1,0:T(8,128)(2,1)} %collective-permute-done.refs_1_, bf16[256,2560]{1,0:T(8,128)(2,1)} %collective-permute-done.1.refs_2_, ...), custom_call_target="tpu_custom_call" | custom-call | flops 21474836480 | bytes 20971520 | tf_op jit(solution)/shard_map/place/pallas_call | solution.py:141
  183.8 22.3 %collective-permute-done.10.refs_2_ = bf16[256,2560]{1,0:T(8,128)(2,1)S(1)} collective-permute-done((bf16[256,2560]{1,0:T(8,128)(2,1)}, bf16[256,2560]{1,0:T(8,128)(2,1)S(1)}, u32[]{:S(2)}, u32[]{:S(2)}) %collective-permute-start.10) | collective-permute-done | bytes 1310752 | tf_op jit(solution)/shard_map/ppermute | solution.py:513
  207.6 34.4 %qkv.2 = (bf16[3,512,640]{2,1,0:T(8,128)(2,1)}, bf16[3,512,640]{2,1,0:T(8,128)(2,1)}, bf16[3,640,512]{2,1,0:T(8,128)(2,1)}, bf16[512,2560]{1,0:T(8,128)(2,1)}) custom-call(s32[2]{0:T(128)} %pad_add_fusion.1.info_ref, bf16[1,2560]{1,0:T(2,128)(2,1)} %broadcast_in_dim.73.g_ref, bf16[4,512,128]{2,1,0:T(8,128)(2,1)} %get-tuple-element.17.mask_ref, ...), custom_call_target="tpu_custom_call" | custom-call | flops 15099494400 | bytes 25559040 | tf_op jit(solution)/shard_map/qkv/pallas_call | solution.py:248
  243.7 1.3 collective-permute-start.14
  247.1 2.2 collective-permute-start.16
  249.4 12.1 %collective-permute-done.14.refs_1_ = bf16[128,2560]{1,0:T(8,128)(2,1)S(1)} collective-permute-done((bf16[128,2560]{1,0:T(8,128)(2,1)S(1)}, bf16[128,2560]{1,0:T(8,128)(2,1)S(1)}, u32[]{:S(2)}, u32[]{:S(2)}) %collective-permute-start.14) | collective-permute-done | bytes 655392 | tf_op jit(solution)/shard_map/ppermute | solution.py:513
  261.4 2.5 collective-permute-done.15.refs_2_
  263.9 10.7 %collective-permute-done.16.refs_3_ = bf16[128,2560]{1,0:T(8,128)(2,1)S(1)} collective-permute-done((bf16[128,2560]{1,0:T(8,128)(2,1)S(1)}, bf16[128,2560]{1,0:T(8,128)(2,1)S(1)}, u32[]{:S(2)}, u32[]{:S(2)}) %collective-permute-start.16) | collective-permute-done | bytes 655392 | tf_op jit(solution)/shard_map/ppermute | solution.py:513
  275.5 17.6 %qkv.3 = (bf16[1,512,640]{2,1,0:T(8,128)(2,1)}, bf16[1,512,640]{2,1,0:T(8,128)(2,1)}, bf16[1,640,512]{2,1,0:T(8,128)(2,1)}) custom-call(s32[2]{0:T(128)} %pad_add_fusion.1.info_ref, bf16[1,2560]{1,0:T(2,128)(2,1)} %broadcast_in_dim.73.g_ref, bf16[4,512,128]{2,1,0:T(8,128)(2,1)} %get-tuple-element.17.mask_ref, f32[4,512,128]{2,1,0:T(8,128)} %pad_maximum_fusion.cos_ref, ...), custom_call_target="tpu_custom_call" | custom-call | flops 5033164800 | bytes 15073280 | tf_op jit(solution)/shard_map/qkv/pallas_call | solution.py:248
  297.9 26.9 %attend.3 = bf16[4,512,256]{2,1,0:T(8,128)(2,1)} custom-call(s32[5]{0:T(128)} %pad_add_fusion.2.info_ref, bf16[3,512,640]{2,1,0:T(8,128)(2,1)} %get-tuple-element.20.refs_0_, bf16[1,512,640]{2,1,0:T(8,128)(2,1)} %get-tuple-element.21.refs_1_, bf16[3,512,640]{2,1,0:T(8,128)(2,1)} %get-tuple-element.22.refs_2_, ...), custom_call_target="tpu_custom_call" | custom-call | flops 5368709120 | bytes 5242880 | tf_op jit(solution)/shard_map/attend/pallas_call | solution.py:387
  324.8 2.0 slice_bitcast_fusion.4
  326.8 1.9 collective-permute-start.24
  328.6 38.7 %attend.2 = bf16[4,512,384]{2,1,0:T(8,128)(2,1)} custom-call(s32[5]{0:T(128)} %pad_add_fusion.2.info_ref, bf16[3,512,640]{2,1,0:T(8,128)(2,1)} %get-tuple-element.20.refs_0_, bf16[1,512,640]{2,1,0:T(8,128)(2,1)} %get-tuple-element.21.refs_1_, bf16[3,512,640]{2,1,0:T(8,128)(2,1)} %get-tuple-element.22.refs_2_, ...), custom_call_target="tpu_custom_call" | custom-call | flops 8053063680 | bytes 7864320 | tf_op jit(solution)/shard_map/attend/pallas_call | solution.py:387
  367.3 2.3 slice_bitcast_fusion
  369.6 2.8 collective-permute-start.21
  372.4 1.5 collective-permute-start.23
  373.9 2.6 collective-permute-start.25
  377.2 25.5 %collective-permute-done.25.refs_6_ = bf16[512,256]{1,0:T(8,128)(2,1)S(1)} collective-permute-done((bf16[512,256]{1,0:T(8,128)(2,1)S(1)}, bf16[512,256]{1,0:T(8,128)(2,1)S(1)}, u32[]{:S(2)}, u32[]{:S(2)}) %collective-permute-start.25) | collective-permute-done | bytes 262176 | tf_op jit(solution)/shard_map/ppermute | solution.py:513
  403.9 16.6 %oproj.1 = (bf16[512,2560]{1,0:T(8,128)(2,1)}, bf16[512,2560]{1,0:T(8,128)(2,1)}) custom-call(s32[2]{0:T(128)} %pad_add_fusion.1.info_ref, bf16[512,384]{1,0:T(8,128)(2,1)} %get-tuple-element.34.refs_0_, bf16[512,384]{1,0:T(8,128)(2,1)} %copy-done.27, bf16[512,384]{1,0:T(8,128)(2,1)} %copy-done.28, bf16[512,384]{1,0:T(8,128)(2,1)} %copy-done.29, ...), custom_call_target="tpu_custom_call" | custom-call | flops 6710886400 | bytes 13107200 | tf_op jit(solution)/shard_map/oproj/pallas_call | solution.py:435
  420.5 65.9 %mlp.1 = bf16[512,2560]{1,0:T(8,128)(2,1)} custom-call(bf16[512,2560]{1,0:T(8,128)(2,1)} %get-tuple-element.27.h_ref, bf16[512,2560]{1,0:T(8,128)(2,1)} %get-tuple-element.28.b_ref, bf16[2560,6912]{1,0:T(8,128)(2,1)} %wg_ref.1, bf16[2560,6912]{1,0:T(8,128)(2,1)} %wu_ref.1, bf16[6912,2560]{1,0:T(8,128)(2,1)} %wd_ref.1), custom_call_target="tpu_custom_call" | custom-call | flops 54358179840 | bytes 106168320 | tf_op jit(solution)/shard_map/mlp/pallas_call | solution.py:476
  (135 shorter events, 29.6 us)
Async XLA Ops:
  5.2 38.0 %copy-start.16 = (s32[256]{0:T(256)S(1)}, s32[256]{0:T(256)}, u32[]{:S(2)}) copy-start(s32[256]{0:T(256)} %param.25) | copy-start | bytes 3076
  5.2 38.0 %copy-start.10 = (s32[3,512]{1,0:T(4,128)S(1)}, s32[3,512]{1,0:T(4,128)}, u32[]{:S(2)}) copy-start(s32[3,512]{1,0:T(4,128)} %param.26) | copy-start | bytes 18436
  5.2 86.0 %copy-start = (bf16[512,2560]{1,0:T(8,128)(2,1)S(1)}, bf16[512,2560]{1,0:T(8,128)(2,1)}, u32[]{:S(2)}) copy-start(bf16[512,2560]{1,0:T(8,128)(2,1)} %refs_0_) | copy-start | bytes 7864324
  41.1 55.9 %collective-permute-start = (bf16[256,2560]{1,0:T(8,128)(2,1)}, bf16[256,2560]{1,0:T(8,128)(2,1)}, u32[]{:S(2)}, u32[]{:S(2)}) collective-permute-start(bf16[256,2560]{1,0:T(8,128)(2,1)} %merger.1.refs_0_), channel_id=1, source_target_pairs={{0,6},{1,7},{2,0},{3,1},{4,2},{5,3},{6,4},{7,5},{8,14},{9,15},{10,... | collective-permute-start | bytes 3932168 | tf_op jit(solution)/shard_map/ppermute | solution.py:513
  41.5 51.8 %collective-permute-start.1 = (bf16[256,2560]{1,0:T(8,128)(2,1)}, bf16[256,2560]{1,0:T(8,128)(2,1)}, u32[]{:S(2)}, u32[]{:S(2)}) collective-permute-start(bf16[256,2560]{1,0:T(8,128)(2,1)} %merger.1.refs_0_), channel_id=1, source_target_pairs={{0,2},{1,3},{2,4},{3,5},{4,6},{5,7},{6,0},{7,1},{8,10},{9,11},{10,... | collective-permute-start | bytes 3932168 | tf_op jit(solution)/shard_map/ppermute | solution.py:513
  93.0 34.5 %copy-start.14 = (bf16[2560]{0:T(1024)(128)(2,1)S(1)}, bf16[2560]{0:T(1024)(128)(2,1)}, u32[]{:S(2)}) copy-start(bf16[2560]{0:T(1024)(128)(2,1)} %param.40) | copy-start | bytes 15364
  93.0 31.9 %collective-permute-start.11 = (bf16[256,2560]{1,0:T(8,128)(2,1)}, bf16[256,2560]{1,0:T(8,128)(2,1)S(1)}, u32[]{:S(2)}, u32[]{:S(2)}) collective-permute-start(bf16[256,2560]{1,0:T(8,128)(2,1)} %get-tuple-element.30), channel_id=1, source_target_pairs={{0,2},{1,3},{2,4},{3,5},{4,6},{5,7},{6,0},{7,1},{8,10},{9,11},{10,... | collective-permute-start | bytes 3932168 | tf_op jit(solution)/shard_map/ppermute | solution.py:513
  93.1 53.9 %collective-permute-start.4 = (bf16[256,2560]{1,0:T(8,128)(2,1)S(1)}, bf16[256,2560]{1,0:T(8,128)(2,1)}, u32[]{:S(2)}, u32[]{:S(2)}) collective-permute-start(bf16[256,2560]{1,0:T(8,128)(2,1)S(1)} %copy-done.6), channel_id=1, source_target_pairs={{0,1},{1,0},{2,3},{3,2},{4,5},{5,4},{6,7},{7,6},{8,9},{9,8},{10,11... | collective-permute-start | bytes 3932168 | tf_op jit(solution)/shard_map/ppermute | solution.py:516
  94.5 38.4 %collective-permute-start.2 = (bf16[128,2560]{1,0:T(8,128)(2,1)S(1)}, bf16[128,2560]{1,0:T(8,128)(2,1)S(1)}, u32[]{:S(2)}, u32[]{:S(2)}) collective-permute-start(bf16[128,2560]{1,0:T(8,128)(2,1)S(1)} %slice.107), channel_id=1, source_target_pairs={{0,2},{1,3},{2,4},{3,5},{4,6},{5,7},{6,0},{7,1},{8,10},{9,11},{10,... | collective-permute-start | bytes 1966088 | tf_op jit(solution)/shard_map/ppermute | solution.py:513
  98.2 34.7 %collective-permute-start.3 = (bf16[128,2560]{1,0:T(8,128)(2,1)S(1)}, bf16[128,2560]{1,0:T(8,128)(2,1)S(1)}, u32[]{:S(2)}, u32[]{:S(2)}) collective-permute-start(bf16[128,2560]{1,0:T(8,128)(2,1)S(1)} %slice.108), channel_id=1, source_target_pairs={{0,6},{1,7},{2,0},{3,1},{4,2},{5,3},{6,4},{7,5},{8,14},{9,15},{10,... | collective-permute-start | bytes 1966088 | tf_op jit(solution)/shard_map/ppermute | solution.py:513
  98.3 49.9 %collective-permute-start.5 = (bf16[256,2560]{1,0:T(8,128)(2,1)}, bf16[256,2560]{1,0:T(8,128)(2,1)S(1)}, u32[]{:S(2)}, u32[]{:S(2)}) collective-permute-start(bf16[256,2560]{1,0:T(8,128)(2,1)} %collective-permute-done.refs_1_), channel_id=1, source_target_pairs={{0,1},{1,0},{2,3},{3,2},{4,5},{5,4},{6,7},{7,6},{8,9},{9,8},{10,11... | collective-permute-start | bytes 3932168 | tf_op jit(solution)/shard_map/ppermute | solution.py:516
  124.9 25.0 %collective-permute-start.6 = (bf16[256,2560]{1,0:T(8,128)(2,1)}, bf16[256,2560]{1,0:T(8,128)(2,1)S(1)}, u32[]{:S(2)}, u32[]{:S(2)}) collective-permute-start(bf16[256,2560]{1,0:T(8,128)(2,1)} %collective-permute-done.1.refs_2_), channel_id=1, source_target_pairs={{0,1},{1,0},{2,3},{3,2},{4,5},{5,4},{6,7},{7,6},{8,9},{9,8},{10,11... | collective-permute-start | bytes 3932168 | tf_op jit(solution)/shard_map/ppermute | solution.py:516
  132.9 18.4 %collective-permute-start.7 = (bf16[128,2560]{1,0:T(8,128)(2,1)S(1)}, bf16[128,2560]{1,0:T(8,128)(2,1)S(1)}, u32[]{:S(2)}, u32[]{:S(2)}) collective-permute-start(bf16[128,2560]{1,0:T(8,128)(2,1)S(1)} %collective-permute-done.2.refs_3_), channel_id=1, source_target_pairs={{0,1},{1,0},{2,3},{3,2},{4,5},{5,4},{6,7},{7,6},{8,9},{9,8},{10,11... | collective-permute-start | bytes 1966088 | tf_op jit(solution)/shard_map/ppermute | solution.py:516
  132.9 19.2 %collective-permute-start.8 = (bf16[128,2560]{1,0:T(8,128)(2,1)S(1)}, bf16[128,2560]{1,0:T(8,128)(2,1)S(1)}, u32[]{:S(2)}, u32[]{:S(2)}) collective-permute-start(bf16[128,2560]{1,0:T(8,128)(2,1)S(1)} %collective-permute-done.3.refs_4_), channel_id=1, source_target_pairs={{0,1},{1,0},{2,3},{3,2},{4,5},{5,4},{6,7},{7,6},{8,9},{9,8},{10,11... | collective-permute-start | bytes 1966088 | tf_op jit(solution)/shard_map/ppermute | solution.py:516
  147.0 36.8 %collective-permute-start.9 = (bf16[256,2560]{1,0:T(8,128)(2,1)}, bf16[256,2560]{1,0:T(8,128)(2,1)S(1)}, u32[]{:S(2)}, u32[]{:S(2)}) collective-permute-start(bf16[256,2560]{1,0:T(8,128)(2,1)} %get-tuple-element.30), channel_id=1, source_target_pairs={{0,6},{1,7},{2,0},{3,1},{4,2},{5,3},{6,4},{7,5},{8,14},{9,15},{10,... | collective-permute-start | bytes 3932168 | tf_op jit(solution)/shard_map/ppermute | solution.py:513
  148.2 57.9 %collective-permute-start.10 = (bf16[256,2560]{1,0:T(8,128)(2,1)}, bf16[256,2560]{1,0:T(8,128)(2,1)S(1)}, u32[]{:S(2)}, u32[]{:S(2)}) collective-permute-start(bf16[256,2560]{1,0:T(8,128)(2,1)} %get-tuple-element.29), channel_id=1, source_target_pairs={{0,6},{1,7},{2,0},{3,1},{4,2},{5,3},{6,4},{7,5},{8,14},{9,15},{10,... | collective-permute-start | bytes 3932168 | tf_op jit(solution)/shard_map/ppermute | solution.py:513
  151.1 55.0 %collective-permute-start.12 = (bf16[256,2560]{1,0:T(8,128)(2,1)}, bf16[256,2560]{1,0:T(8,128)(2,1)S(1)}, u32[]{:S(2)}, u32[]{:S(2)}) collective-permute-start(bf16[256,2560]{1,0:T(8,128)(2,1)} %get-tuple-element.29), channel_id=1, source_target_pairs={{0,2},{1,3},{2,4},{3,5},{4,6},{5,7},{6,0},{7,1},{8,10},{9,11},{10,... | collective-permute-start | bytes 3932168 | tf_op jit(solution)/shard_map/ppermute | solution.py:513
  151.4 95.8 %collective-permute-start.13 = (bf16[128,2560]{1,0:T(8,128)(2,1)}, bf16[128,2560]{1,0:T(8,128)(2,1)}, u32[]{:S(2)}, u32[]{:S(2)}) collective-permute-start(bf16[128,2560]{1,0:T(8,128)(2,1)} %slice.112), channel_id=1, source_target_pairs={{0,2},{1,3},{2,4},{3,5},{4,6},{5,7},{6,0},{7,1},{8,10},{9,11},{10,... | collective-permute-start | bytes 1966088 | tf_op jit(solution)/shard_map/ppermute | solution.py:513
  242.0 54.4 %collective-permute-start.17 = (bf16[3,512,640]{2,1,0:T(8,128)(2,1)}, bf16[3,512,640]{2,1,0:T(8,128)(2,1)S(1)}, u32[]{:S(2)}, u32[]{:S(2)}) collective-permute-start(bf16[3,512,640]{2,1,0:T(8,128)(2,1)} %get-tuple-element.22.refs_2_), channel_id=1, source_target_pairs={{0,1},{1,0},{2,3},{3,2},{4,5},{5,4},{6,7},{7,6},{8,9},{9,8},{10,11... | collective-permute-start | bytes 5898248 | tf_op jit(solution)/shard_map/ppermute | solution.py:516
  242.1 54.3 %collective-permute-start.19 = (bf16[3,640,512]{2,1,0:T(8,128)(2,1)}, bf16[3,640,512]{2,1,0:T(8,128)(2,1)}, u32[]{:S(2)}, u32[]{:S(2)}) collective-permute-start(bf16[3,640,512]{2,1,0:T(8,128)(2,1)} %get-tuple-element.24.refs_6_), channel_id=1, source_target_pairs={{0,1},{1,0},{2,3},{3,2},{4,5},{5,4},{6,7},{7,6},{8,9},{9,8},{10,11... | collective-permute-start | bytes 5898248 | tf_op jit(solution)/shard_map/ppermute | solution.py:516
  243.7 17.7 %collective-permute-start.14 = (bf16[128,2560]{1,0:T(8,128)(2,1)S(1)}, bf16[128,2560]{1,0:T(8,128)(2,1)S(1)}, u32[]{:S(2)}, u32[]{:S(2)}) collective-permute-start(bf16[128,2560]{1,0:T(8,128)(2,1)S(1)} %slice.113), channel_id=1, source_target_pairs={{0,6},{1,7},{2,0},{3,1},{4,2},{5,3},{6,4},{7,5},{8,14},{9,15},{10,... | collective-permute-start | bytes 1966088 | tf_op jit(solution)/shard_map/ppermute | solution.py:513
  246.2 17.7 %collective-permute-start.15 = (bf16[128,2560]{1,0:T(8,128)(2,1)S(1)}, bf16[128,2560]{1,0:T(8,128)(2,1)S(1)}, u32[]{:S(2)}, u32[]{:S(2)}) collective-permute-start(bf16[128,2560]{1,0:T(8,128)(2,1)S(1)} %slice.114), channel_id=1, source_target_pairs={{0,2},{1,3},{2,4},{3,5},{4,6},{5,7},{6,0},{7,1},{8,10},{9,11},{10,... | collective-permute-start | bytes 1966088 | tf_op jit(solution)/shard_map/ppermute | solution.py:513
  247.1 46.6 %copy-start.17 = (s32[3]{0:T(128)S(1)}, s32[3]{0:T(128)}, u32[]{:S(2)}) copy-start(s32[3]{0:T(128)} %param.27) | copy-start | bytes 40
  247.1 27.5 %collective-permute-start.16 = (bf16[128,2560]{1,0:T(8,128)(2,1)S(1)}, bf16[128,2560]{1,0:T(8,128)(2,1)S(1)}, u32[]{:S(2)}, u32[]{:S(2)}) collective-permute-start(bf16[128,2560]{1,0:T(8,128)(2,1)S(1)} %slice.115), channel_id=1, source_target_pairs={{0,6},{1,7},{2,0},{3,1},{4,2},{5,3},{6,4},{7,5},{8,14},{9,15},{10,... | collective-permute-start | bytes 1966088 | tf_op jit(solution)/shard_map/ppermute | solution.py:513
  293.1 2.4 collective-permute-start.18
  293.2 3.2 collective-permute-start.20
  326.8 49.8 %collective-permute-start.24 = (bf16[512,256]{1,0:T(8,128)(2,1)S(1)}, bf16[512,256]{1,0:T(8,128)(2,1)S(1)}, u32[]{:S(2)}, u32[]{:S(2)}) collective-permute-start(bf16[512,256]{1,0:T(8,128)(2,1)S(1)} %get-tuple-element.37), channel_id=1, source_target_pairs={{0,2},{1,3},{2,4},{3,5},{4,6},{5,7},{6,0},{7,1},{8,10},{9,11},{10,... | collective-permute-start | bytes 786440 | tf_op jit(solution)/shard_map/ppermute | solution.py:513
  369.6 33.1 %collective-permute-start.21 = (bf16[512,384]{1,0:T(8,128)(2,1)S(1)}, bf16[512,384]{1,0:T(8,128)(2,1)S(1)}, u32[]{:S(2)}, u32[]{:S(2)}) collective-permute-start(bf16[512,384]{1,0:T(8,128)(2,1)S(1)} %get-tuple-element.33), channel_id=1, source_target_pairs={{0,2},{1,3},{2,4},{3,5},{4,6},{5,7},{6,0},{7,1},{8,10},{9,11},{10,... | collective-permute-start | bytes 1179656 | tf_op jit(solution)/shard_map/ppermute | solution.py:513
  372.4 30.3 %collective-permute-start.22 = (bf16[512,384]{1,0:T(8,128)(2,1)S(1)}, bf16[512,384]{1,0:T(8,128)(2,1)S(1)}, u32[]{:S(2)}, u32[]{:S(2)}) collective-permute-start(bf16[512,384]{1,0:T(8,128)(2,1)S(1)} %get-tuple-element.32), channel_id=1, source_target_pairs={{0,6},{1,7},{2,0},{3,1},{4,2},{5,3},{6,4},{7,5},{8,14},{9,15},{10,... | collective-permute-start | bytes 1179656 | tf_op jit(solution)/shard_map/ppermute | solution.py:513
  372.4 30.3 %collective-permute-start.23 = (bf16[512,384]{1,0:T(8,128)(2,1)S(1)}, bf16[512,384]{1,0:T(8,128)(2,1)S(1)}, u32[]{:S(2)}, u32[]{:S(2)}) collective-permute-start(bf16[512,384]{1,0:T(8,128)(2,1)S(1)} %get-tuple-element.31), channel_id=1, source_target_pairs={{0,4},{1,5},{2,6},{3,7},{4,0},{5,1},{6,2},{7,3},{8,12},{9,13},{10,... | collective-permute-start | bytes 1179656 | tf_op jit(solution)/shard_map/ppermute | solution.py:513
  373.9 28.8 %collective-permute-start.25 = (bf16[512,256]{1,0:T(8,128)(2,1)S(1)}, bf16[512,256]{1,0:T(8,128)(2,1)S(1)}, u32[]{:S(2)}, u32[]{:S(2)}) collective-permute-start(bf16[512,256]{1,0:T(8,128)(2,1)S(1)} %get-tuple-element.36), channel_id=1, source_target_pairs={{0,6},{1,7},{2,0},{3,1},{4,2},{5,3},{6,4},{7,5},{8,14},{9,15},{10,... | collective-permute-start | bytes 786440 | tf_op jit(solution)/shard_map/ppermute | solution.py:513
  376.5 26.2 %collective-permute-start.26 = (bf16[512,256]{1,0:T(8,128)(2,1)S(1)}, bf16[512,256]{1,0:T(8,128)(2,1)S(1)}, u32[]{:S(2)}, u32[]{:S(2)}) collective-permute-start(bf16[512,256]{1,0:T(8,128)(2,1)S(1)} %get-tuple-element.35), channel_id=1, source_target_pairs={{0,4},{1,5},{2,6},{3,7},{4,0},{5,1},{6,2},{7,3},{8,12},{9,13},{10,... | collective-permute-start | bytes 786440 | tf_op jit(solution)/shard_map/ppermute | solution.py:513
  (28 other events, 248.2 us)
